TPU v7x, 256 devices: a 8x8x2 block of a 8x8x16 slice. The times are simulated.
256 devices in a mesh: pop: 2 (over z), dp: 2 (over core), tensor: 64 (over y, x).
Axes of the slice: x: 8, y: 8, z: 2, core: 2. Of those that a mesh axis runs over, the one named last changes fastest.
The devices are a block of a 8x8x16 slice.
Arguments:
- tokens: bfloat16 [1024, 16384], P(('pop', 'dp'), 'tensor'), parts along dimension 0, may hold values from -6 to 6
- weight: bfloat16 [16384, 26624], P('dp', 'tensor'), may hold values from -0.046875 to 0.046875
- adapter_in: bfloat16 [8, 16384, 64], P(('pop', 'dp'), 'tensor'), parts along dimension 0, may hold values from -0.046875 to 0.046875
- adapter_out: bfloat16 [8, 64, 26624], P(('pop', 'dp'), None, 'tensor'), parts along dimension 0, may hold values from -0.375 to 0.375
- cotangent: bfloat16 [1024, 26624], P(('pop', 'dp'), 'tensor'), parts along dimension 0, may hold values from -0.59765625 to 0.59765625
- member_blocks: int32 [8], P('pop'), parts along dimension 0, may hold values from 0 to 3, as said below
- block_live: int32 [8], P(('pop', 'dp')), parts along dimension 0, may hold values from 1 to 128, as said below
Outputs:
- hidden: bfloat16 [1024, 26624], P(('pop', 'dp'), 'tensor'), parts along dimension 0
- input_gradient: bfloat16 [1024, 16384], P(('pop', 'dp'), 'tensor'), parts along dimension 0
- down_factor_gradient: float32 [8, 16384, 64], P(('pop', 'dp'), 'tensor'), parts along dimension 0
- up_factor_gradient: float32 [8, 64, 26624], P(('pop', 'dp'), None, 'tensor'), parts along dimension 0
There are 2 independent parts, one for each index of `pop`. A program takes and returns all parts, laid end to end along the dimension named above; an argument that names none is the same for every part. Nothing has to cross between parts.
Inputs may be any that keep to these rules, and one draw needn't show every extreme that they name: `member_blocks`: the number of 128-token blocks of each member; the counts sum to 4 and the blocks come in order of member. `block_live`: the live tokens stand at the start of each block; every block but the last one of its member is full.
All inputs are finite; a program needn't handle non-finite values.
Results may differ from a plain program's by a relative error of at most 0.003.
Values may be sent and summed in bfloat16 or wider, within the bound.
A program may use at most 128 MiB of HBM per device.

v0:
```python
import functools
import math

import jax
import jax.numpy as jnp
from jax import lax
from jax.sharding import Mesh
from jax.sharding import PartitionSpec as P

MEMBERS = 4
BLOCK = 128
TENSOR = ("tensor_0", "tensor_1")


adapter_scale = 0.5


def side_by_side(arrays, axis, dim, along):
    widths = [math.prod(a.shape[along:]) for a in arrays]
    both = jnp.concatenate(
        [a.reshape(*a.shape[:along], w) for a, w in zip(arrays, widths)], axis=along
    )
    result = lax.all_gather(both, axis, axis=dim, tiled=True)
    pieces = jnp.split(result, [sum(widths[:k]) for k in range(1, len(widths))], axis=along)
    return tuple(
        (b.reshape(*result.shape[:along], *a.shape[along:]) for a, b in zip(arrays, pieces))
    )


def over_axes(x, axes):
    return functools.reduce(lax.psum, axes, x)


def own_rows(subtotal, axes):
    for axis in axes:
        subtotal = lax.psum_scatter(subtotal, axis, scatter_dimension=0, tiled=True)
    return subtotal


def in_blocks(x, dim, length):
    before, after = (x.shape[:dim], x.shape[dim + 1 :])
    return jnp.moveaxis(x.reshape(*before, length, -1, *after), dim, 0)


def sum_at_owner(x, axis, dim):
    pieces = in_blocks(x, dim, lax.axis_size(axis))
    arrived = lax.all_to_all(pieces, axis, split_axis=0, concat_axis=0, tiled=True)
    return arrived.sum(axis=0)


def in_one_piece(arrays, axis, dim, along):
    widths = [math.prod(a.shape[along:]) for a in arrays]
    both = jnp.concatenate(
        [a.reshape(*a.shape[:along], w) for a, w in zip(arrays, widths)], axis=along
    )
    result = sum_at_owner(both, axis, dim)
    pieces = jnp.split(result, [sum(widths[:k]) for k in range(1, len(widths))], axis=along)
    return tuple(
        (b.reshape(*result.shape[:along], *a.shape[along:]) for a, b in zip(arrays, pieces))
    )


def block_members(member_blocks, first, count):
    ends = jnp.cumsum(member_blocks)
    blocks = first + jnp.arange(count, dtype=jnp.int32)
    return jnp.sum((ends[None, :] <= blocks[:, None]).astype(jnp.int32), axis=1)


def member_table(members, count):
    owners = jnp.arange(count, dtype=jnp.int32)
    return (members[:, None] == owners[None, :]).astype(jnp.float32)


def member_grads(member_lookup, token_blocks, grad_blocks, lowin_blocks, lowback_blocks):
    down_outer_product = jnp.einsum(
        "btk,btr->bkr", token_blocks, lowback_blocks, preferred_element_type=jnp.float32
    )
    up_outer_product = jnp.einsum(
        "btr,btf->brf", lowin_blocks, grad_blocks, preferred_element_type=jnp.float32
    )
    down_factor_gradient = adapter_scale * jnp.einsum(
        "gw,gsd->wsd", member_lookup, down_outer_product, precision=lax.Precision.HIGHEST
    )
    up_factor_gradient = adapter_scale * jnp.einsum(
        "jg,juy->guy", member_lookup, up_outer_product, precision=lax.Precision.HIGHEST
    )
    return (down_factor_gradient, up_factor_gradient)


def local(tokens, weight, adapter_in, adapter_out, cotangent, member_blocks, block_live):
    token_rows, width_local = tokens.shape
    hidden_local = weight.shape[1]
    blocks_here = token_rows // BLOCK
    first_block = lax.axis_index("dp") * blocks_here
    members = block_members(member_blocks, first_block, blocks_here)
    offsets = jnp.arange(BLOCK, dtype=jnp.int32)
    active_member_mask = (
        (offsets[None, :] < block_live[:, None]).astype(jnp.bfloat16).reshape(token_rows, 1)
    )
    features = lax.all_gather(tokens, TENSOR, axis=1, tiled=True)
    down_all, up_all = side_by_side((adapter_in, adapter_out), "dp", 0, 1)
    piece = lax.all_gather(weight, "dp", axis=0, tiled=True)
    total = jnp.dot(features, piece, preferred_element_type=jnp.float32)
    chosen_in = jnp.take(down_all, members, axis=0)
    chosen_out = jnp.take(up_all, members, axis=0)
    token_blocks = tokens.reshape(blocks_here, BLOCK, width_local)
    masked = cotangent * active_member_mask
    grad_blocks = masked.reshape(blocks_here, BLOCK, hidden_local)
    part_in = jnp.einsum(
        "btk,bkr->btr", token_blocks, chosen_in, preferred_element_type=jnp.float32
    )
    part_back = jnp.einsum(
        "btf,brf->btr", grad_blocks, chosen_out, preferred_element_type=jnp.float32
    )
    sum_in, sum_back = (over_axes(part_in, TENSOR), over_axes(part_back, TENSOR))
    low_in = sum_in.astype(jnp.bfloat16)
    low_back = sum_back.astype(jnp.bfloat16)
    raised_hidden = jnp.einsum(
        "btr,brf->btf", low_in, chosen_out, preferred_element_type=jnp.float32
    )
    raised_hidden = raised_hidden.reshape(token_rows, hidden_local)
    hidden = (
        active_member_mask.astype(jnp.float32) * (total + adapter_scale * raised_hidden)
    ).astype(jnp.bfloat16)
    combined_sum = own_rows(
        lax.dot_general(
            piece, masked, (((1,), (1,)), ((), ())), preferred_element_type=jnp.float32
        ),
        TENSOR,
    )
    reduced_hidden = jnp.einsum(
        "btr,bkr->btk", low_back, chosen_in, preferred_element_type=jnp.float32
    )
    reduced_hidden = reduced_hidden.reshape(token_rows, width_local)
    input_gradient = (combined_sum.T + adapter_scale * reduced_hidden).astype(jnp.bfloat16)
    member_lookup = member_table(members, MEMBERS)
    down_factor_gradient, up_factor_gradient = member_grads(
        member_lookup, token_blocks, grad_blocks, low_in, low_back
    )
    down_factor_gradient, up_factor_gradient = in_one_piece(
        (down_factor_gradient, up_factor_gradient), "dp", 0, 1
    )
    return (hidden, input_gradient, down_factor_gradient, up_factor_gradient)


def solution(mesh):
    finer = Mesh(
        mesh.devices.reshape(mesh.shape["pop"], mesh.shape["dp"], 8, 8),
        ("pop", "dp", "tensor_0", "tensor_1"),
    )
    placed = (
        P(("pop", "dp"), TENSOR),
        P("dp", TENSOR),
        P(("pop", "dp"), TENSOR, None),
        P(("pop", "dp"), None, TENSOR),
        P(("pop", "dp"), TENSOR),
        P("pop"),
        P(("pop", "dp")),
    )
    return jax.shard_map(
        local,
        mesh=finer,
        in_specs=placed,
        out_specs=(
            P(("pop", "dp"), TENSOR),
            P(("pop", "dp"), TENSOR),
            P(("pop", "dp"), TENSOR, None),
            P(("pop", "dp"), None, TENSOR),
        ),
        check_vma=False,
    )
```

profile of v0, /device:TPU:514, one launch (start us, length us, event | category | flops | bytes accessed | tf_op | source)
XLA Modules:
  0.0 391.7 jit_solution(14345710955920300912)
XLA Ops:
  8.0 0.1 all-gather.6.cloned.1.call-start
  8.1 0.7 all-gather.6.cloned.1.call-update
  8.8 0.1 all-reduce.5.cloned.1.call-start
  8.9 1.1 reshape.125
  10.0 1.0 copy.30
  11.0 0.2 reshape.124
  11.2 0.2 maximum_bitcast_fusion
  11.3 2.1 all-gather
  13.4 0.1 reshape.150
  13.6 0.1 split.17
  13.7 0.4 reshape.128
  14.1 0.3 reshape.126
  14.4 0.1 copy.31
  14.5 0.8 reduce-window.8
  15.4 0.2 fusion.20
  15.6 0.6 gather_fusion.1
  16.1 0.6 gather_fusion
  16.7 0.7 fusion.29
  17.4 1.7 convolution_bitcast_fusion.2
  19.2 1.8 fusion.7
  21.0 0.1 all-reduce.5.cloned.1.call-update
  21.1 0.1 reduce-scatter.3.cloned.1.call-start
  21.1 40.1 %all-gather.6.cloned.1.call-done = bf16[16384,416]{0,1:T(8,128)(2,1)} async-done(((bf16[8192,416]{0,1:T(8,128)(2,1)}), bf16[16384,416]{0,1:T(8,128)(2,1)}) %all-gather.6.cloned.1.call-update) | async-done | bytes 13631504 | tf_op jit(solution)/shard_map/all_gather | solution.py:102
  61.2 15.3 %convolution_bitcast_fusion = f32[16384,256]{0,1:T(8,128)} fusion(bf16[16384,416]{0,1:T(8,128)(2,1)} %all-gather.6.cloned.1.call-done, bf16[256,416]{0,1:T(8,128)(2,1)} %param.11, bf16[256]{0:T(256)(128)(2,1)S(1)} %get-tuple-element.21), kind=kOutput, calls=%fused_computation.2 | convolution fusion | flops 3489767424 | bytes 30622208 | tf_op jit(solution)/shard_map/dot_general | solution.py:126
  76.5 0.0 copy-start
  76.5 0.0 copy-start.1
  76.5 0.1 reduce-scatter.3.cloned.1.call-update
  76.5 0.1 all-gather.4.cloned.1.call-start
  76.6 0.6 all-gather.4.cloned.1.call-update
  77.2 0.1 reduce-scatter.5.cloned.1.call-start
  77.3 72.2 %all-reduce.5.cloned.1.call-done = (f32[2,128,64]{1,2,0:T(8,128)}, f32[2,128,64]{1,2,0:T(8,128)}) async-done(((f32[2,128,64]{1,2,0:T(8,128)}, f32[2,128,64]{1,2,0:T(8,128)}), (f32[2,128,64]{1,2,0:T(8,128)}, f32[2,128,64]{1,2,0:T(8,128)})) %all-reduce.5.cloned.1.call-update) | async-done | bytes 131088 | tf_op jit(solution)/shard_map/psum | solution.py:31
  149.5 31.5 %all-reduce.6 = (bf16[2,128,64]{1,2,0:T(8,128)(2,1)S(1)}, bf16[2,128,64]{1,2,0:T(8,128)(2,1)S(1)}) all-reduce(f32[2,128,64]{1,2,0:T(8,128)} %get-tuple-element.18, f32[2,128,64]{1,2,0:T(8,128)} %get-tuple-element.19), channel_id=1, replica_groups=mesh['pop'=2,'dp'=2,'tensor_0'=8,'tensor_1'=8] {'tensor_1'}, use_global_device_ids=true, to_apply=%region_3.4 | all-reduce | flops 32768 | bytes 196608 | tf_op jit(solution)/shard_map/psum | solution.py:31
  181.0 0.0 copy-done
  181.0 0.2 fusion.5
  181.2 0.9 convolution_multiply_fusion
  182.1 0.2 copy.38
  182.3 0.5 concatenate.13
  182.8 0.0 copy-done.1
  182.8 0.1 convolution_bitcast_fusion.1
  183.0 0.5 convolution_multiply_fusion.2
  183.5 0.2 copy.35
  183.7 0.3 concatenate.12
  184.0 154.9 %reduce-scatter.3.cloned.1.call-done = f32[2048,256]{0,1:T(8,128)} async-done(((f32[16384,256]{0,1:T(8,128)}), f32[2048,256]{0,1:T(8,128)}) %reduce-scatter.3.cloned.1.call-update) | async-done | bytes 2097168 | tf_op jit(solution)/shard_map/reduce_scatter | solution.py:36
  338.9 0.1 reduce-scatter.5.cloned.1.call-update
  339.0 0.3 pad_maximum_fusion
  339.3 4.3 %all_to_all.5 = f32[2,2,43008]{2,1,0:T(2,128)S(1)} all-to-all(f32[2,2,43008]{2,1,0:T(2,128)S(1)} %pad_maximum_fusion), channel_id=1, replica_groups=mesh['pop'=2,'dp'=2,'tensor_0'=8,'tensor_1'=8] {'dp'}, dimensions={0} | all-to-all | bytes 1376256 | tf_op jit(solution)/shard_map/all_to_all | solution.py:47
  343.5 0.6 reduce_sum.22
  344.2 0.2 reshape.130
  344.4 0.8 copy.39
  345.2 1.0 reshape.131
  346.1 0.3 fusion
  346.5 0.2 convolution_multiply_fusion.3
  346.7 0.0 all-gather.4.cloned.1.call-done
  346.8 11.9 %fusion.2 = bf16[256,416]{0,1:T(8,128)(2,1)} fusion(bf16[256,16384]{1,0:T(8,128)(2,1)} %all-gather.4.cloned.1.call-done, bf16[16384,416]{0,1:T(8,128)(2,1)} %all-gather.6.cloned.1.call-done, f32[2,52,8,128]{3,2,1,0:T(8,128)S(1)} %fusion, f32[256]{0:T(256)S(1)} %get-tuple-element.20), kind=kOutput, calls=%fused_computation.8 | convolution fusion | flops 3489980416 | bytes 22660096 | tf_op jit(solution)/shard_map/dot_general | solution.py:103
  358.6 24.3 %reduce-scatter.5.cloned.1.call-done = f32[256,256]{0,1:T(8,128)} async-done(((f32[2048,256]{0,1:T(8,128)}), f32[256,256]{0,1:T(8,128)}) %reduce-scatter.5.cloned.1.call-update) | async-done | bytes 262160 | tf_op jit(solution)/shard_map/reduce_scatter | solution.py:36
  383.0 1.6 fusion.3
  (7 shorter events, 0.1 us)
Async XLA Ops:
  8.0 53.2 %all-gather.6.cloned.1.call-start = ((), (), s32[]{:S(2)}) async-start(), calls=%async_computation.4 | async-start | bytes 20447232 | tf_op jit(solution)/shard_map/all_gather | solution.py:102
  8.8 140.6 %all-reduce.5.cloned.1.call-start = ((), (), s32[]{:S(2)}) async-start(), calls=%async_computation.7 | async-start | bytes 262144 | tf_op jit(solution)/shard_map/psum | solution.py:31
  21.1 317.8 %reduce-scatter.3.cloned.1.call-start = ((), (), s32[]{:S(2)}) async-start(), calls=%async_computation.5 | async-start | bytes 18874368 | tf_op jit(solution)/shard_map/reduce_scatter | solution.py:36
  76.5 104.5 %copy-start = (bf16[256,416]{0,1:T(8,128)(2,1)S(1)}, bf16[256,416]{0,1:T(8,128)(2,1)}, u32[]{:S(2)}) copy-start(bf16[256,416]{0,1:T(8,128)(2,1)} %param.11) | copy-start | bytes 638980
  76.5 106.3 %copy-start.1 = (bf16[256,256]{1,0:T(8,128)(2,1)S(1)}, bf16[256,256]{1,0:T(8,128)(2,1)}, u32[]{:S(2)}) copy-start(bf16[256,256]{1,0:T(8,128)(2,1)} %param.7) | copy-start | bytes 393220
  76.5 270.2 %all-gather.4.cloned.1.call-start = ((), (), s32[]{:S(2)}) async-start(), calls=%async_computation.3 | async-start | bytes 8519680 | tf_op jit(solution)/shard_map/all_gather | solution.py:100
  77.2 305.8 %reduce-scatter.5.cloned.1.call-start = ((), (), s32[]{:S(2)}) async-start(), calls=%async_computation.6 | async-start | bytes 2359296 | tf_op jit(solution)/shard_map/reduce_scatter | solution.py:36
Sparse Core Ops, SparseCore 0:
  10.7 50.4 all-gather.5
  64.2 85.2 all-reduce.4
  152.1 186.7 reduce-scatter.2
  341.3 41.5 reduce-scatter.4
Sparse Core Ops, SparseCore 1:
  79.5 125.5 all-gather.3
where the time goes:
time: 392 us
  waiting for transfers between devices  293 us (75%)
  blocking collectives  37.9 us (10%)
  matrix products  33 us (8%)
  between operations  15.5 us (4%)
  local copies, waits for them, and re-layouts  7.59 us (2%)
  other arithmetic  4.47 us (1%)
    reduce_scatter x2, waiting for transfers between devices, own_rows(): subtotal = lax.psum_scatter(subtotal, axis, scatter_dimension=0, tiled=True)  179 us
    psum x1, waiting for transfers between devices, over_axes(): return functools.reduce(lax.psum, axes, x)  72.2 us
    all_gather x1, waiting for transfers between devices, local(): piece = lax.all_gather(weight, 'dp', axis=0, tiled=True)  40.1 us
    psum x1, blocking collectives, over_axes(): return functools.reduce(lax.psum, axes, x)  31.5 us
    dot_general x1, matrix products, local(): lax.dot_general(piece, masked, (((1,), (1,)), ((), ())), preferred_elemen...  15.3 us
    dot_general x1, matrix products, local(): total = jnp.dot(features, piece, preferred_element_type=jnp.float32)  11.9 us
  transfers between devices with their start and end apart: 5, of which 4 were waited for; matrix products, arithmetic and copies ran while one was open for 11% of the time, Pallas kernels for 0%

commit v1 on v0

v1 whole, which is shorter than its diff:
```python
import functools
import math

import jax
import jax.numpy as jnp
from jax import lax
from jax.experimental import pallas as pl
from jax.experimental.pallas import tpu as pltpu
from jax.sharding import Mesh
from jax.sharding import PartitionSpec as P

BLOCK = 128
SCALE = 0.5
MESH = pl.DeviceIdType.MESH
ROW, COL, CORE = "tensor_0", "tensor_1", "dp"
F32, BF16 = jnp.float32, jnp.bfloat16

NN = (((1,), (0,)), ((), ()))
NT = (((1,), (1,)), ((), ()))
TN = (((0,), (0,)), ((), ()))


def dot(a, b, dims):
    return lax.dot_general(a, b, dims, preferred_element_type=F32)


LANES, SUBLANES = 128, 8
UNIT = 2.0**21
TOP = 32760.0


def halves(v):
    return [v[:, k : k + LANES] for k in range(0, v.shape[1], LANES)]


def encode(v):
    groups = [h.reshape(-1, SUBLANES, LANES) for h in halves(v)]
    largest = functools.reduce(jnp.maximum, [jnp.max(jnp.abs(q), axis=0) for q in groups])
    scale = (largest * UNIT).astype(jnp.int32) + 1
    by = (TOP * UNIT) / scale.astype(F32)
    out = []
    for q in groups:
        code = (q * by[None]).astype(jnp.int32)
        mid = code.shape[0] // 2
        pair = (code[:mid] << 16) | (code[mid:] & 0xFFFF)
        out.append(pair.reshape(-1, LANES))
    return jnp.concatenate([*out, scale], axis=0)


def decode(code):
    scale = code[-SUBLANES:].astype(F32) * (1.0 / (TOP * UNIT))
    body = code[:-SUBLANES]
    mid = body.shape[0] // 2
    out = []
    for k in range(2):
        pair = body[k * mid : (k + 1) * mid].reshape(-1, SUBLANES, LANES)
        both = jnp.concatenate([pair >> 16, (pair << 16) >> 16], axis=0)
        out.append((both.astype(F32) * scale[None]).reshape(-1, LANES))
    return jnp.concatenate(out, axis=1)


def kernel(
    n,
    mb,
    bl,
    tok_hbm,
    w_hbm,
    ain_hbm,
    aout_hbm,
    cot,
    hidden,
    igrad,
    dgrad,
    ugrad,
    g,
    w,
    p,
    rb,
    r2,
    masked,
    acc,
    adt,
    ain,
    aout,
    cin,
    cout,
    part,
    xbuf,
    ybuf,
    low,
    usend,
    dsend,
    urecv,
    drecv,
    ag1_s,
    ag1_r,
    ag2_s,
    ag2_r,
    rs1_s,
    rs1_r,
    rs2_s,
    rs2_r,
    own_sem,
    w_sem,
    wx_s,
    wx_r,
    ad_sem,
    adx_s,
    adx_r,
    xs,
    xr,
    ys,
    yr,
    zs,
    zr,
    gx_s,
    gx_r,
):
    half = n // 2
    ticks = n + half
    early, middle, late = n // 4, n // 2, 3 * n // 4
    y, x, d = lax.axis_index(ROW), lax.axis_index(COL), lax.axis_index(CORE)
    mate = {CORE: 1 - d}
    me = y * n + x
    chunks = n * n
    members = ain.shape[0]
    owned = members // 2
    own_chunks = w_hbm.shape[0]
    pieces = w_sem.shape[0]
    piece = own_chunks // pieces
    rank = ain.shape[2]
    minor_axis, major_axis = (COL, ROW), (ROW, COL)
    minor_at, major_at = (x, y), (y, x)

    def chunk(c, major, minor):
        return major * n + minor if c == 0 else minor * n + major

    def wrap(v):
        return lax.rem(v + 2 * n, n)

    def remote(src, dst, ss, rs, to):
        return pltpu.make_async_remote_copy(
            src_ref=src, dst_ref=dst, send_sem=ss, recv_sem=rs, device_id=to, device_id_type=MESH
        )

    def landed(dst, sem):
        pltpu.make_async_copy(dst, dst, sem).wait()

    for c in range(2):
        pltpu.make_async_copy(tok_hbm.at[c], g.at[c, me], own_sem.at[c]).start()
    barrier = pltpu.get_barrier_semaphore()
    for k in range(1, n):
        pl.semaphore_signal(barrier, inc=1, device_id={COL: wrap(x + k)}, device_id_type=MESH)
        pl.semaphore_signal(barrier, inc=1, device_id={ROW: wrap(y + k)}, device_id_type=MESH)
    pl.semaphore_signal(barrier, inc=1, device_id=mate, device_id_type=MESH)

    def ad_local(k):
        hbm, vm = ((ain_hbm, ain), (aout_hbm, aout))[k]
        return pltpu.make_async_copy(hbm, vm.at[pl.ds(d * owned, owned)], ad_sem.at[k])

    def ad_remote(k):
        hbm, vm = ((ain_hbm, ain), (aout_hbm, aout))[k]
        return remote(hbm, vm.at[pl.ds(d * owned, owned)], adx_s.at[k], adx_r.at[k], mate)

    def w_local(q):
        src = w_hbm.at[pl.ds(q * piece, piece)]
        return pltpu.make_async_copy(src, w.at[pl.ds(d * own_chunks + q * piece, piece)], w_sem.at[q])

    def w_remote(q):
        src = w_hbm.at[pl.ds(q * piece, piece)]
        return remote(src, w.at[pl.ds(d * own_chunks + q * piece, piece)], wx_s.at[q], wx_r.at[q], mate)

    for k in range(2):
        ad_local(k).start()
    for q in range(pieces):
        w_local(q).start()
    for c in range(2):
        landed(g.at[c, me], own_sem.at[c])
    pl.semaphore_wait(barrier, 2 * (n - 1) + 1)

    def minor_offset(j):
        back = lax.div(j + 1, 2)
        return jnp.where(lax.rem(j, 2) == 1, -back, lax.div(j, 2))

    def ag1_copy(c, j, right):
        src = chunk(c, major_at[c], wrap(minor_at[c] + minor_offset(j)))
        lands = jnp.where(j == 0, 1 if right else 2, j + 2)
        to = {minor_axis[c]: wrap(minor_at[c] + (1 if right else -1))}
        return remote(g.at[c, src], g.at[c, src], ag1_s.at[c, lands], ag1_r.at[c, lands], to)

    def ag1_step(j):
        for c in range(2):
            src = chunk(c, major_at[c], wrap(minor_at[c] + minor_offset(j)))

            @pl.when(j >= 1)
            def _(c=c, src=src):
                landed(g.at[c, src], ag1_r.at[c, j])

            @pl.when(jnp.logical_or(j == 0, jnp.logical_and(lax.rem(j, 2) == 1, j + 2 < n)))
            def _(c=c):
                ag1_copy(c, j, True).start()

            @pl.when(jnp.logical_and(lax.rem(j, 2) == 0, j + 2 < n))
            def _(c=c):
                ag1_copy(c, j, False).start()

    def ag2_copy(c, e, j, s):
        way = 1 - 2 * e
        t = chunk(c, wrap(major_at[c] - way * s), wrap(minor_at[c] + minor_offset(j)))
        to = {major_axis[c]: wrap(major_at[c] + way)}
        return remote(g.at[c, t], g.at[c, t], ag2_s.at[c, e, j, s], ag2_r.at[c, e, j, s], to)

    def ag2_landed(c, e, j, s):
        t = chunk(c, wrap(major_at[c] - (1 - 2 * e) * s), wrap(minor_at[c] + minor_offset(j)))
        landed(g.at[c, t], ag2_r.at[c, e, j, s - 1])

    def is_long(e, j):
        return lax.rem(j, 2) == e

    def live_stream(j):
        return jnp.logical_and(j >= 0, j < n)

    def ag_tick(tick):
        @pl.when(tick < n)
        def _():
            ag1_step(tick)

        for s in range(half + 1):
            j = tick - s

            @pl.when(live_stream(j))
            def _(j=j, s=s):
                for c in range(2):
                    for e in range(2):
                        if s < half:
                            if s > 0:
                                ag2_landed(c, e, j, s)
                            if s < half - 1:
                                ag2_copy(c, e, j, s).start()
                            else:

                                @pl.when(is_long(e, j))
                                def _(c=c, e=e):
                                    ag2_copy(c, e, j, s).start()
                        else:

                            @pl.when(is_long(e, j))
                            def _(c=c, e=e):
                                ag2_landed(c, e, j, s)

    def dest_offset(i):
        ahead = lax.div(n - i, 2)
        back = lax.div(n - 1 - i, 2)
        return jnp.where(lax.rem(i, 2) == 0, ahead, -back)

    def hops(e, i):
        return jnp.where(is_long(e, i), half, half - 1)

    def rs1_chunk(c, e, i, s):
        far = (1 - 2 * e) * (hops(e, i) - s)
        return chunk(c, wrap(major_at[c] + far), wrap(minor_at[c] + dest_offset(i)))

    def rs1_copy(c, e, i, s):
        t = rs1_chunk(c, e, i, s)
        to = {major_axis[c]: wrap(major_at[c] + 1 - 2 * e)}
        return remote(p.at[c, t], rb.at[c, e, i, s], rs1_s.at[c, e, i, s], rs1_r.at[c, e, i, s], to)

    def rs1_add_send(c, e, i, s):
        t = rs1_chunk(c, e, i, s)
        p[c, t] = encode(decode(p[c, t]) + decode(rb[c, e, i, s - 1]))
        rs1_copy(c, e, i, s).start()

    def rs2_copy(c, i, right):
        t = chunk(c, major_at[c], wrap(minor_at[c] + dest_offset(i)))
        to = {minor_axis[c]: wrap(minor_at[c] + (1 if right else -1))}
        return remote(p.at[c, t], r2.at[c, i], rs2_s.at[c, i], rs2_r.at[c, i], to)

    def rs1_done(c, i):
        t = chunk(c, major_at[c], wrap(minor_at[c] + dest_offset(i)))
        total = decode(p[c, t])
        for e in range(2):
            total = total + decode(rb[c, e, i, hops(e, i) - 1])
        return t, total

    def rs2_step(i):
        for c in range(2):

            @pl.when(i < 2)
            def _(c=c):
                t, total = rs1_done(c, i)
                p[c, t] = encode(total)

            @pl.when(jnp.logical_and(i >= 2, i < n - 1))
            def _(c=c):
                landed(r2.at[c, i - 2], rs2_r.at[c, i - 2])
                t, total = rs1_done(c, i)
                p[c, t] = encode(total + decode(r2[c, i - 2]))

            @pl.when(jnp.logical_and(i < n - 1, lax.rem(i, 2) == 0))
            def _(c=c):
                rs2_copy(c, i, True).start()

            @pl.when(jnp.logical_and(i < n - 1, lax.rem(i, 2) == 1))
            def _(c=c):
                rs2_copy(c, i, False).start()

            @pl.when(i == n - 1)
            def _(c=c):
                t, total = rs1_done(c, i)
                total = total + adt[c]
                for k in (n - 3, n - 2):
                    landed(r2.at[c, k], rs2_r.at[c, k])
                    total = total + decode(r2[c, k])
                igrad[c] = total.astype(BF16)

    def rs_tick(tick):
        for s in range(half + 1):
            i = tick - s

            @pl.when(live_stream(i))
            def _(i=i, s=s):
                for c in range(2):
                    for e in range(2):
                        if s == 0:
                            rs1_copy(c, e, i, s).start()
                        elif s < half - 1:
                            landed(rb.at[c, e, i, s - 1], rs1_r.at[c, e, i, s - 1])
                            rs1_add_send(c, e, i, s)
                        elif s == half - 1:
                            landed(rb.at[c, e, i, s - 1], rs1_r.at[c, e, i, s - 1])

                            @pl.when(is_long(e, i))
                            def _(c=c, e=e):
                                rs1_add_send(c, e, i, s)
                        else:

                            @pl.when(is_long(e, i))
                            def _(c=c, e=e):
                                landed(rb.at[c, e, i, s - 1], rs1_r.at[c, e, i, s - 1])

                if s == half:
                    rs2_step(i)

    def member_of(b):
        end, count = jnp.int32(0), jnp.int32(0)
        for m in range(members):
            end = end + mb[m]
            count = count + jnp.where(end <= d * 2 + b, 1, 0)
        return count

    def weight_of(b, m):
        return jnp.where(member_of(b) == m, F32(1.0), F32(0.0))

    def live_rows(b):
        at = lax.broadcasted_iota(jnp.int32, (BLOCK, cot.shape[2]), 0)
        return jnp.where(at < bl[b], F32(1.0), F32(0.0))

    def rows(b):
        return pl.ds(b * BLOCK, BLOCK)

    def mask_step():
        for b in range(2):
            masked[rows(b)] = (cot[b].astype(F32) * live_rows(b)).astype(BF16)

    def low_rank_start():
        for k in range(2):
            ad_local(k).wait()
            ad_remote(k).wait_recv()
        for b in range(2):
            a, o = weight_of(b, 0) * ain[0].astype(F32), weight_of(b, 0) * aout[0].astype(F32)
            for m in range(1, members):
                a = a + weight_of(b, m) * ain[m].astype(F32)
                o = o + weight_of(b, m) * aout[m].astype(F32)
            cin[b], cout[b] = a.astype(BF16), o.astype(BF16)
        tall = part.shape[1]
        for b in range(2):
            into = dot(g[b, me], cin[b], NN)
            back = dot(masked[rows(b)], cout[b], NT)
            both = jnp.concatenate([into, back], axis=1)
            each = BLOCK // tall
            part[pl.ds(b * each, each)] = both.reshape(each, tall, 2 * rank)
        xbuf[x] = part[x]

    def x_copy(k):
        to = wrap(x + k)
        return remote(part.at[to], xbuf.at[x], xs.at[k], xr.at[k], {COL: to})

    def y_copy(k):
        return remote(ybuf.at[y], ybuf.at[y], ys.at[k], yr.at[k], {ROW: wrap(y + k)})

    def z_copy(k):
        return remote(low.at[x], low.at[x], zs.at[k], zr.at[k], {COL: wrap(x + k)})

    def total_of(ref):
        total = ref[0]
        for k in range(1, n):
            total = total + ref[k]
        return total

    def x_done():
        for k in range(1, n):
            landed(xbuf.at[wrap(x - k)], xr.at[k])
        ybuf[y] = total_of(xbuf)

    def y_done():
        for k in range(1, n):
            landed(ybuf.at[wrap(y - k)], yr.at[k])
        low[x] = total_of(ybuf).astype(BF16)

    def low_of(b):
        each = n // 2
        both = low[pl.ds(b * each, each)].reshape(BLOCK, 2 * rank)
        return both[:, :rank], both[:, rank:]

    def g_copy(k):
        src, dst = ((usend, urecv), (dsend, drecv))[k]
        return remote(src, dst, gx_s.at[k], gx_r.at[k], mate)

    def z_done():
        for k in range(1, n):
            landed(low.at[wrap(x - k)], zr.at[k])
        ups, downs = [], []
        for b in range(2):
            into, back = low_of(b)
            ups.append(SCALE * dot(into, masked[rows(b)], TN))
            downs.append(SCALE * dot(g[b, me], back, TN))
        for q in range(owned):
            theirs, mine = (1 - d) * owned + q, d * owned + q
            usend[q] = weight_of(0, theirs) * ups[0] + weight_of(1, theirs) * ups[1]
            dsend[q] = weight_of(0, theirs) * downs[0] + weight_of(1, theirs) * downs[1]
            ugrad[q] = weight_of(0, mine) * ups[0] + weight_of(1, mine) * ups[1]
            dgrad[q] = weight_of(0, mine) * downs[0] + weight_of(1, mine) * downs[1]

    def terms_step():
        for b in range(2):
            into, back = low_of(b)
            acc[rows(b)] = SCALE * dot(into, cout[b], NN)
            adt[b] = SCALE * dot(back, cin[b], NT)

    def grads_done():
        for k in range(2):
            g_copy(k).wait_recv()
        for q in range(owned):
            ugrad[q] = ugrad[q] + urecv[q]
            dgrad[q] = dgrad[q] + drecv[q]

    def back_chunk(k):
        t = lax.rem(d * own_chunks + k, chunks)
        out = dot(masked[...], w[t], NT)
        for b in range(2):
            p[b, t] = encode(out[b * BLOCK : (b + 1) * BLOCK])

    def front_chunk(t):
        rows_in = jnp.concatenate([g[0, t], g[1, t]], axis=0)
        acc[...] += dot(rows_in, w[t], NN)

    def hidden_step():
        for b in range(2):
            hidden[b] = (acc[rows(b)] * live_rows(b)).astype(BF16)

    def some(body, first, last):
        lax.fori_loop(first, last, lambda k, z: (body(k), z)[1], 0)

    rs_from = n
    last = rs_from + ticks - 1
    back_from, back_ticks = early, rs_from - early
    back_each = -(-chunks // back_ticks)
    front_from, front_ticks = ticks, last - 1 - ticks
    front_each = -(-chunks // front_ticks)

    def every_tick(tick, carry):
        @pl.when(tick < ticks)
        def _():
            ag_tick(tick)

        @pl.when(tick >= rs_from)
        def _():
            rs_tick(tick - rs_from)

        @pl.when(tick == 0)
        def _():
            for k in range(2):
                ad_remote(k).start()
            for q in range(pieces):
                w_remote(q).start()
            mask_step()
            low_rank_start()
            for k in range(1, n):
                x_copy(k).start()

        @pl.when(tick == early)
        def _():
            x_done()
            for k in range(1, n):
                y_copy(k).start()
            for q in range(pieces):
                w_local(q).wait()

        @pl.when(tick == middle)
        def _():
            y_done()
            for k in range(1, n):
                z_copy(k).start()
            for q in range(pieces):
                theirs = w.at[pl.ds((1 - d) * own_chunks + q * piece, piece)]
                landed(theirs, wx_r.at[q])

        @pl.when(tick == late)
        def _():
            z_done()
            for k in range(2):
                g_copy(k).start()
            terms_step()

        @pl.when(tick == rs_from + 1)
        def _():
            grads_done()

        @pl.when(jnp.logical_and(tick >= back_from, tick < back_from + back_ticks))
        def _():
            first = (tick - back_from) * back_each
            some(back_chunk, first, jnp.minimum(first + back_each, chunks))

        @pl.when(jnp.logical_and(tick >= front_from, tick < front_from + front_ticks))
        def _():
            first = (tick - front_from) * front_each
            some(front_chunk, first, jnp.minimum(first + front_each, chunks))

        @pl.when(tick == front_from + front_ticks)
        def _():
            hidden_step()

        return carry

    lax.fori_loop(0, last + 1, every_tick, 0)

    for k in range(2):
        ad_remote(k).wait_send()
        g_copy(k).wait_send()
    for q in range(pieces):
        w_remote(q).wait_send()
    for k in range(1, n):
        x_copy(k).wait_send()
        y_copy(k).wait_send()
        z_copy(k).wait_send()

    def sent(src, sem):
        pltpu.make_async_copy(src, src, sem).wait()

    def drain(j, carry):
        @pl.when(j >= 1)
        def _():
            for c in range(2):
                sent(g.at[c, 0], ag1_s.at[c, j])

        @pl.when(j < n - 1)
        def _():
            for c in range(2):
                sent(p.at[c, 0], rs2_s.at[c, j])

        for c in range(2):
            for e in range(2):
                for s in range(half - 1):
                    sent(g.at[c, 0], ag2_s.at[c, e, j, s])
                    sent(p.at[c, 0], rs1_s.at[c, e, j, s])

                @pl.when(is_long(e, j))
                def _(c=c, e=e):
                    sent(g.at[c, 0], ag2_s.at[c, e, j, half - 1])
                    sent(p.at[c, 0], rs1_s.at[c, e, j, half - 1])

        return carry

    lax.fori_loop(0, n, drain, 0)


def local(n, tokens, weight, adapter_in, adapter_out, cotangent, member_blocks, block_live):
    token_rows, width = tokens.shape
    depth, hidden_width = weight.shape
    blocks = token_rows // BLOCK
    owned, _, rank = adapter_in.shape
    members = 2 * owned
    half = n // 2
    tall = token_rows // n
    chunks = n * n
    vmem, anywhere, smem = (
        pl.BlockSpec(memory_space=s) for s in (pltpu.VMEM, pl.ANY, pltpu.SMEM)
    )
    pieces = 4
    coded = BLOCK * width // (2 * LANES) + SUBLANES
    dma = lambda *shape: pltpu.SemaphoreType.DMA(shape)
    both_ways = (2, 2, n, half)
    out = pl.pallas_call(
        functools.partial(kernel, n),
        out_shape=(
            jax.ShapeDtypeStruct((blocks, BLOCK, hidden_width), BF16),
            jax.ShapeDtypeStruct((blocks, BLOCK, width), BF16),
            jax.ShapeDtypeStruct((owned, width, rank), F32),
            jax.ShapeDtypeStruct((owned, rank, hidden_width), F32),
        ),
        in_specs=[smem, smem, anywhere, anywhere, anywhere, anywhere, vmem],
        out_specs=(vmem,) * 4,
        scratch_shapes=[
            pltpu.VMEM((blocks, chunks, BLOCK, width), BF16),
            pltpu.VMEM((chunks, width, hidden_width), BF16),
            pltpu.VMEM((blocks, chunks, coded, LANES), jnp.int32),
            pltpu.VMEM((*both_ways, coded, LANES), jnp.int32),
            pltpu.VMEM((2, n - 1, coded, LANES), jnp.int32),
            pltpu.VMEM((token_rows, hidden_width), BF16),
            pltpu.VMEM((token_rows, hidden_width), F32),
            pltpu.VMEM((blocks, BLOCK, width), F32),
            pltpu.VMEM((members, width, rank), BF16),
            pltpu.VMEM((members, rank, hidden_width), BF16),
            pltpu.VMEM((blocks, width, rank), BF16),
            pltpu.VMEM((blocks, rank, hidden_width), BF16),
            pltpu.VMEM((n, tall, 2 * rank), F32),
            pltpu.VMEM((n, tall, 2 * rank), F32),
            pltpu.VMEM((n, tall, 2 * rank), F32),
            pltpu.VMEM((n, tall, 2 * rank), BF16),
            pltpu.VMEM((owned, rank, hidden_width), F32),
            pltpu.VMEM((owned, width, rank), F32),
            pltpu.VMEM((owned, rank, hidden_width), F32),
            pltpu.VMEM((owned, width, rank), F32),
            dma(2, n),
            dma(2, n),
            dma(*both_ways),
            dma(*both_ways),
            dma(*both_ways),
            dma(*both_ways),
            dma(2, n),
            dma(2, n),
            dma(2),
            dma(pieces),
            dma(pieces),
            dma(pieces),
            dma(2),
            dma(2),
            dma(2),
            dma(n),
            dma(n),
            dma(n),
            dma(n),
            dma(n),
            dma(n),
            dma(2),
            dma(2),
        ],
        compiler_params=pltpu.CompilerParams(
            collective_id=0, has_side_effects=True, vmem_limit_bytes=62 * 2**20
        ),
        name="step",
    )(
        member_blocks,
        block_live,
        tokens.reshape(blocks, BLOCK, width),
        weight.reshape(depth // width, width, hidden_width),
        adapter_in,
        adapter_out,
        cotangent.reshape(blocks, BLOCK, hidden_width),
    )
    return (
        out[0].reshape(token_rows, hidden_width),
        out[1].reshape(token_rows, width),
        out[2],
        out[3],
    )


def solution(mesh):
    n = math.isqrt(mesh.shape["tensor"])
    tensor = (ROW, COL)
    finer = Mesh(
        mesh.devices.reshape(mesh.shape["pop"], mesh.shape["dp"], n, n), ("pop", CORE, ROW, COL)
    )
    return jax.shard_map(
        functools.partial(local, n),
        mesh=finer,
        in_specs=(
            P(("pop", "dp"), tensor),
            P("dp", tensor),
            P(("pop", "dp"), tensor, None),
            P(("pop", "dp"), None, tensor),
            P(("pop", "dp"), tensor),
            P("pop"),
            P(("pop", "dp")),
        ),
        out_specs=(
            P(("pop", "dp"), tensor),
            P(("pop", "dp"), tensor),
            P(("pop", "dp"), tensor, None),
            P(("pop", "dp"), None, tensor),
        ),
        check_vma=False,
    )
```

time: 392 us -> 158 us (0.40)
  waiting for transfers between devices: 293 us -> 0 us
  Pallas kernels: 0 us -> 136 us
  blocking collectives: 37.9 us -> 0 us
  matrix products: 33 us -> 0 us
  between operations: 15.5 us -> 0.64 us
  local copies, waits for them, and re-layouts: 7.59 us -> 20.9 us
  other arithmetic: 4.47 us -> 0 us
    reduce_scatter x2 -> x0, waiting for transfers between devices: 179 us -> none  [own_rows(): subtotal = lax.psum_scatter(subtotal, axis, scatter_dimension=0, tiled=True)]
    pallas_call x0 -> x1, Pallas kernels: none -> 136 us  [local(): pl.pallas_call(functools.partial(kernel, n), out_shape=(jax.ShapeDtypeStr...]
    psum x1 -> x0, waiting for transfers between devices: 72.2 us -> none  [over_axes(): return functools.reduce(lax.psum, axes, x)]
    all_gather x2 -> x0, waiting for transfers between devices: 40.1 us -> none  [the longest x1 40.1 us: local(): piece = lax.all_gather(weight, 'dp', axis=0, tiled=True)]
    dot_general x10 -> x0, matrix products: 33 us -> none  [the longest x1 15.3 us: local(): lax.dot_general(piece, masked, (((1,), (1,)), ((), ())), preferred_elemen...]
    psum x1 -> x0, blocking collectives: 31.5 us -> none  [over_axes(): return functools.reduce(lax.psum, axes, x)]
    unnamed x7, local copies, waits for them, and re-layouts: 1.87 us -> 20.9 us
    all_to_all x1 -> x0, blocking collectives: 4.28 us -> none  [sum_at_owner(): lax.all_to_all(pieces, axis, split_axis=0, concat_axis=0, tiled=True)]
  transfers between devices with their start and end apart: 5 -> 0, of which waited for: 4 -> 0; matrix products, arithmetic and copies ran while one was open for 11% -> 0% of each run, Pallas kernels for 0% -> 0%
where the time goes in v1:
time: 158 us; the launch traced here: 157 us
  Pallas kernels  136 us (86%)
  local copies, waits for them, and re-layouts  20.9 us (13%)
    pallas_call x1, Pallas kernels, local(): pl.pallas_call(functools.partial(kernel, n), out_shape=(jax.ShapeDtypeStr...  136 us
    unnamed x7, local copies, waits for them, and re-layouts  20.9 us

profile of v1, /device:TPU:514, one launch (start us, length us, event | category | flops | bytes accessed | tf_op | source)
XLA Modules:
  0.0 157.2 jit_solution(11147950015428663400)
XLA Ops:
  0.6 1.6 %copy.13.ain_hbm = bf16[2,256,64]{2,1,0:T(8,128)(2,1)} copy(bf16[2,256,64]{1,2,0:T(8,128)(2,1)} %param.9) | data formatting | bytes 131072 | tf_op args[2]
  2.2 1.8 %copy.12 = bf16[256,416]{1,0:T(8,128)(2,1)} copy(bf16[256,416]{0,1:T(8,128)(2,1)} %param.11) | data formatting | bytes 425984 | tf_op args[4]
  4.0 10.8 %copy.11 = bf16[8192,416]{1,0:T(8,128)(2,1)} copy(bf16[8192,416]{0,1:T(8,128)(2,1)} %param.8) | data formatting | bytes 13631488 | tf_op args[1]
  14.8 135.6 %step.1 = (bf16[2,128,416]{2,1,0:T(8,128)(2,1)}, bf16[2,128,256]{2,1,0:T(8,128)(2,1)}, f32[2,256,64]{2,1,0:T(8,128)}, f32[2,64,416]{2,1,0:T(8,128)}) custom-call(s32[4]{0:T(128)} %mb.1, s32[2]{0:T(128)} %bl.1, bf16[2,128,256]{2,1,0:T(8,128)(2,1)} %bitcast.8, bf16[32,256,416]{2,1,0:T(8,128)(2,1)} %bitcast.5, bf16[2,256,64]{2,1,0:T(8,128)(2,1)} %copy.13.ain_hbm, ...), custom_call_target="tpu_custom_call" | custom-call | tf_op jit(solution)/shard_map/step/pallas_call | solution.py:593
  150.5 1.8 %copy.14 = bf16[256,416]{0,1:T(8,128)(2,1)} copy(bf16[256,416]{1,0:T(8,128)(2,1)} %bitcast.7) | data formatting | bytes 425984
  152.2 1.7 %copy.15 = f32[2,256,64]{1,2,0:T(8,128)} copy(f32[2,256,64]{2,1,0:T(8,128)} %get-tuple-element.14) | data formatting | bytes 262144
  154.0 1.6 copy.18
  155.5 1.7 %copy.19 = f32[2,64,416]{2,1,0:T(8,128)} copy(f32[2,64,416]{2,1,0:T(8,128)} %get-tuple-element.23) | data formatting | bytes 425984

commit v2 on v1

--- a/solution.py
+++ b/solution.py
@@ -125,10 +125,12 @@
     chunks = n * n
     members = ain.shape[0]
     owned = members // 2
-    own_chunks = w_hbm.shape[0]
+    width = g.shape[3]
+    own_depth = w_hbm.shape[1]
+    own_chunks = own_depth // width
     pieces = w_sem.shape[0]
-    piece = own_chunks // pieces
-    rank = ain.shape[2]
+    piece = own_depth // pieces
+    rank = ain.shape[1]
     minor_axis, major_axis = (COL, ROW), (ROW, COL)
     minor_at, major_at = (x, y), (y, x)
 
@@ -162,13 +164,19 @@
         hbm, vm = ((ain_hbm, ain), (aout_hbm, aout))[k]
         return remote(hbm, vm.at[pl.ds(d * owned, owned)], adx_s.at[k], adx_r.at[k], mate)
 
+    def w_piece(core, q):
+        return w.at[:, pl.ds(pl.multiple_of(core * own_depth + q * piece, LANES), piece)]
+
     def w_local(q):
-        src = w_hbm.at[pl.ds(q * piece, piece)]
-        return pltpu.make_async_copy(src, w.at[pl.ds(d * own_chunks + q * piece, piece)], w_sem.at[q])
+        src = w_hbm.at[:, pl.ds(q * piece, piece)]
+        return pltpu.make_async_copy(src, w_piece(d, q), w_sem.at[q])
 
     def w_remote(q):
-        src = w_hbm.at[pl.ds(q * piece, piece)]
-        return remote(src, w.at[pl.ds(d * own_chunks + q * piece, piece)], wx_s.at[q], wx_r.at[q], mate)
+        src = w_hbm.at[:, pl.ds(q * piece, piece)]
+        return remote(src, w_piece(d, q), wx_s.at[q], wx_r.at[q], mate)
+
+    def w_chunk(t):
+        return w[:, pl.ds(pl.multiple_of(t * width, LANES), width)]
 
     for k in range(2):
         ad_local(k).start()
@@ -351,8 +359,8 @@
     def weight_of(b, m):
         return jnp.where(member_of(b) == m, F32(1.0), F32(0.0))
 
-    def live_rows(b):
-        at = lax.broadcasted_iota(jnp.int32, (BLOCK, cot.shape[2]), 0)
+    def live(b, shape, dim):
+        at = lax.broadcasted_iota(jnp.int32, shape, dim)
         return jnp.where(at < bl[b], F32(1.0), F32(0.0))
 
     def rows(b):
@@ -360,7 +368,8 @@
 
     def mask_step():
         for b in range(2):
-            masked[rows(b)] = (cot[b].astype(F32) * live_rows(b)).astype(BF16)
+            across = jnp.transpose(cot[:, b * BLOCK : (b + 1) * BLOCK].astype(F32))
+            masked[rows(b)] = (across * live(b, across.shape, 0)).astype(BF16)
 
     def low_rank_start():
         for k in range(2):
@@ -374,7 +383,7 @@
             cin[b], cout[b] = a.astype(BF16), o.astype(BF16)
         tall = part.shape[1]
         for b in range(2):
-            into = dot(g[b, me], cin[b], NN)
+            into = dot(g[b, me], cin[b], NT)
             back = dot(masked[rows(b)], cout[b], NT)
             both = jnp.concatenate([into, back], axis=1)
             each = BLOCK // tall
@@ -423,7 +432,7 @@
         for b in range(2):
             into, back = low_of(b)
             ups.append(SCALE * dot(into, masked[rows(b)], TN))
-            downs.append(SCALE * dot(g[b, me], back, TN))
+            downs.append(SCALE * dot(back, g[b, me], TN))
         for q in range(owned):
             theirs, mine = (1 - d) * owned + q, d * owned + q
             usend[q] = weight_of(0, theirs) * ups[0] + weight_of(1, theirs) * ups[1]
@@ -434,8 +443,9 @@
     def terms_step():
         for b in range(2):
             into, back = low_of(b)
-            acc[rows(b)] = SCALE * dot(into, cout[b], NN)
-            adt[b] = SCALE * dot(back, cin[b], NT)
+            turned = jnp.transpose(into.astype(F32)).astype(BF16)
+            acc[:, b * BLOCK : (b + 1) * BLOCK] = SCALE * dot(cout[b], turned, TN)
+            adt[b] = SCALE * dot(back, cin[b], NN)
 
     def grads_done():
         for k in range(2):
@@ -446,17 +456,18 @@
 
     def back_chunk(k):
         t = lax.rem(d * own_chunks + k, chunks)
-        out = dot(masked[...], w[t], NT)
+        out = dot(masked[...], w_chunk(t), NN)
         for b in range(2):
             p[b, t] = encode(out[b * BLOCK : (b + 1) * BLOCK])
 
     def front_chunk(t):
         rows_in = jnp.concatenate([g[0, t], g[1, t]], axis=0)
-        acc[...] += dot(rows_in, w[t], NN)
+        acc[...] += dot(w_chunk(t), rows_in, NT)
 
     def hidden_step():
         for b in range(2):
-            hidden[b] = (acc[rows(b)] * live_rows(b)).astype(BF16)
+            cols = acc[:, b * BLOCK : (b + 1) * BLOCK]
+            hidden[:, b * BLOCK : (b + 1) * BLOCK] = (cols * live(b, cols.shape, 1)).astype(BF16)
 
     def some(body, first, last):
         lax.fori_loop(first, last, lambda k, z: (body(k), z)[1], 0)
@@ -502,8 +513,7 @@
             for k in range(1, n):
                 z_copy(k).start()
             for q in range(pieces):
-                theirs = w.at[pl.ds((1 - d) * own_chunks + q * piece, piece)]
-                landed(theirs, wx_r.at[q])
+                landed(w_piece(1 - d, q), wx_r.at[q])
 
         @pl.when(tick == late)
         def _():
@@ -574,9 +584,14 @@
     lax.fori_loop(0, n, drain, 0)
 
 
+def hand_over(*refs):
+    for src, dst in zip(refs[:4], refs[4:]):
+        dst[...] = src[...]
+
+
 def local(n, tokens, weight, adapter_in, adapter_out, cotangent, member_blocks, block_live):
     token_rows, width = tokens.shape
-    depth, hidden_width = weight.shape
+    hidden_width = weight.shape[1]
     blocks = token_rows // BLOCK
     owned, _, rank = adapter_in.shape
     members = 2 * owned
@@ -593,34 +608,34 @@
     out = pl.pallas_call(
         functools.partial(kernel, n),
         out_shape=(
-            jax.ShapeDtypeStruct((blocks, BLOCK, hidden_width), BF16),
+            jax.ShapeDtypeStruct((hidden_width, token_rows), BF16),
             jax.ShapeDtypeStruct((blocks, BLOCK, width), BF16),
-            jax.ShapeDtypeStruct((owned, width, rank), F32),
+            jax.ShapeDtypeStruct((owned, rank, width), F32),
             jax.ShapeDtypeStruct((owned, rank, hidden_width), F32),
         ),
         in_specs=[smem, smem, anywhere, anywhere, anywhere, anywhere, vmem],
         out_specs=(vmem,) * 4,
         scratch_shapes=[
             pltpu.VMEM((blocks, chunks, BLOCK, width), BF16),
-            pltpu.VMEM((chunks, width, hidden_width), BF16),
+            pltpu.VMEM((hidden_width, chunks * width), BF16),
             pltpu.VMEM((blocks, chunks, coded, LANES), jnp.int32),
             pltpu.VMEM((*both_ways, coded, LANES), jnp.int32),
             pltpu.VMEM((2, n - 1, coded, LANES), jnp.int32),
             pltpu.VMEM((token_rows, hidden_width), BF16),
-            pltpu.VMEM((token_rows, hidden_width), F32),
+            pltpu.VMEM((hidden_width, token_rows), F32),
             pltpu.VMEM((blocks, BLOCK, width), F32),
-            pltpu.VMEM((members, width, rank), BF16),
+            pltpu.VMEM((members, rank, width), BF16),
             pltpu.VMEM((members, rank, hidden_width), BF16),
-            pltpu.VMEM((blocks, width, rank), BF16),
+            pltpu.VMEM((blocks, rank, width), BF16),
             pltpu.VMEM((blocks, rank, hidden_width), BF16),
             pltpu.VMEM((n, tall, 2 * rank), F32),
             pltpu.VMEM((n, tall, 2 * rank), F32),
             pltpu.VMEM((n, tall, 2 * rank), F32),
             pltpu.VMEM((n, tall, 2 * rank), BF16),
             pltpu.VMEM((owned, rank, hidden_width), F32),
-            pltpu.VMEM((owned, width, rank), F32),
+            pltpu.VMEM((owned, rank, width), F32),
             pltpu.VMEM((owned, rank, hidden_width), F32),
-            pltpu.VMEM((owned, width, rank), F32),
+            pltpu.VMEM((owned, rank, width), F32),
             dma(2, n),
             dma(2, n),
             dma(*both_ways),
@@ -653,15 +668,22 @@
         member_blocks,
         block_live,
         tokens.reshape(blocks, BLOCK, width),
-        weight.reshape(depth // width, width, hidden_width),
-        adapter_in,
+        weight.T,
+        jnp.swapaxes(adapter_in, 1, 2),
         adapter_out,
-        cotangent.reshape(blocks, BLOCK, hidden_width),
+        cotangent.T,
     )
+    out = pl.pallas_call(
+        hand_over,
+        out_shape=tuple(jax.ShapeDtypeStruct(o.shape, o.dtype) for o in out),
+        in_specs=[vmem] * 4,
+        out_specs=(vmem,) * 4,
+        name="hand_over",
+    )(*out)
     return (
-        out[0].reshape(token_rows, hidden_width),
+        out[0].T,
         out[1].reshape(token_rows, width),
-        out[2],
+        jnp.swapaxes(out[2], 1, 2),
         out[3],
     )
 

time: 158 us -> 138 us (0.87)
  local copies, waits for them, and re-layouts: 20.9 us -> 0 us
    unnamed x7 -> x0, local copies, waits for them, and re-layouts: 20.9 us -> none
    pallas_call x0 -> x1, Pallas kernels: none -> 2.06 us  [local(): pl.pallas_call(hand_over, out_shape=tuple((jax.ShapeDtypeStruct(o.shape,...]
where the time goes in v2:
time: 138 us
  Pallas kernels  137 us (99%)
    pallas_call x1, Pallas kernels, local(): pl.pallas_call(functools.partial(kernel, n), out_shape=(jax.ShapeDtypeStr...  135 us

profile of v2, /device:TPU:514, one launch (start us, length us, event | category | flops | bytes accessed | tf_op | source)
XLA Modules:
  0.0 137.9 jit_solution(14817554559253530180)
XLA Ops:
  0.6 135.2 %step.1 = (bf16[416,256]{1,0:T(8,128)(2,1)}, bf16[2,128,256]{2,1,0:T(8,128)(2,1)}, f32[2,64,256]{2,1,0:T(8,128)}, f32[2,64,416]{2,1,0:T(8,128)}) custom-call(s32[4]{0:T(128)} %mb.1, s32[2]{0:T(128)} %bl.1, bf16[2,128,256]{2,1,0:T(8,128)(2,1)} %bitcast.9, bf16[416,8192]{1,0:T(8,128)(2,1)} %bitcast.7, bf16[2,64,256]{2,1,0:T(8,128)(2,1)} %bitcast.10, ...), custom_call_target="tpu_custom_call" | custom-call | tf_op jit(solution)/shard_map/step/pallas_call | solution.py:608
  135.9 2.1 %hand_over.1 = (bf16[416,256]{1,0:T(8,128)(2,1)}, bf16[2,128,256]{2,1,0:T(8,128)(2,1)}, f32[2,64,256]{2,1,0:T(8,128)}, f32[2,64,416]{2,1,0:T(8,128)}) custom-call(bf16[416,256]{1,0:T(8,128)(2,1)} %get-tuple-element.12.refs_0_, bf16[2,128,256]{2,1,0:T(8,128)(2,1)} %get-tuple-element.13.refs_1_, f32[2,64,256]{2,1,0:T(8,128)} %get-tuple-element.14.refs_2_, ...), custom_call_target="tpu_custom_call" | custom-call | tf_op jit(solution)/shard_map/hand_over/pallas_call | solution.py:676

commit v3 on v2

--- a/solution.py
+++ b/solution.py
@@ -24,7 +24,7 @@
     return lax.dot_general(a, b, dims, preferred_element_type=F32)
 
 
-LANES, SUBLANES = 128, 8
+LANES = 128
 UNIT = 2.0**21
 TOP = 32760.0
 
@@ -33,40 +33,44 @@
     return [v[:, k : k + LANES] for k in range(0, v.shape[1], LANES)]
 
 
-def encode(v):
-    groups = [h.reshape(-1, SUBLANES, LANES) for h in halves(v)]
-    largest = functools.reduce(jnp.maximum, [jnp.max(jnp.abs(q), axis=0) for q in groups])
+def put(ref, at, v):
+    parts = halves(v)
+    largest = jnp.max(functools.reduce(jnp.maximum, [jnp.abs(q) for q in parts]), axis=0, keepdims=True)
     scale = (largest * UNIT).astype(jnp.int32) + 1
     by = (TOP * UNIT) / scale.astype(F32)
-    out = []
-    for q in groups:
-        code = (q * by[None]).astype(jnp.int32)
-        mid = code.shape[0] // 2
-        pair = (code[:mid] << 16) | (code[mid:] & 0xFFFF)
-        out.append(pair.reshape(-1, LANES))
-    return jnp.concatenate([*out, scale], axis=0)
-
-
-def decode(code):
-    scale = code[-SUBLANES:].astype(F32) * (1.0 / (TOP * UNIT))
-    body = code[:-SUBLANES]
-    mid = body.shape[0] // 2
+    mid = v.shape[0] // 2
+    for k, q in enumerate(parts):
+        code = (q * by).astype(jnp.int32)
+        ref[(*at, slice(k * mid, (k + 1) * mid))] = (code[:mid] << 16) | (code[mid:] & 0xFFFF)
+    ref[(*at, slice(2 * mid, 2 * mid + 1))] = scale
+
+
+def get(ref, at):
+    mid = (ref.shape[-2] - 1) // 2
+    scale = ref[(*at, slice(2 * mid, 2 * mid + 1))].astype(F32) * (1.0 / (TOP * UNIT))
     out = []
     for k in range(2):
-        pair = body[k * mid : (k + 1) * mid].reshape(-1, SUBLANES, LANES)
+        pair = ref[(*at, slice(k * mid, (k + 1) * mid))]
         both = jnp.concatenate([pair >> 16, (pair << 16) >> 16], axis=0)
-        out.append((both.astype(F32) * scale[None]).reshape(-1, LANES))
+        out.append(both.astype(F32) * scale)
     return jnp.concatenate(out, axis=1)
 
 
 def kernel(
     n,
-    mb,
-    bl,
+    mb_hbm,
+    bl_hbm,
     tok_hbm,
     w_hbm,
     ain_hbm,
     aout_hbm,
+    cot_hbm,
+    hidden_hbm,
+    igrad_hbm,
+    dgrad_hbm,
+    ugrad_hbm,
+    mb,
+    bl,
     cot,
     hidden,
     igrad,
@@ -115,10 +119,15 @@
     zr,
     gx_s,
     gx_r,
+    in_sem,
+    out_sem,
+    here,
 ):
     half = n // 2
     ticks = n + half
-    early, middle, late = n // 4, n // 2, 3 * n // 4
+    early, middle = n // 4, n // 2
+    low_from = early
+    low_to = low_from + 3 * half
     y, x, d = lax.axis_index(ROW), lax.axis_index(COL), lax.axis_index(CORE)
     mate = {CORE: 1 - d}
     me = y * n + x
@@ -148,13 +157,28 @@
     def landed(dst, sem):
         pltpu.make_async_copy(dst, dst, sem).wait()
 
+    barrier = pltpu.get_barrier_semaphore()
+    for step in (1, n - 1):
+        pl.semaphore_signal(barrier, inc=1, device_id={COL: wrap(x + step)}, device_id_type=MESH)
+        pl.semaphore_signal(barrier, inc=1, device_id={ROW: wrap(y + step)}, device_id_type=MESH)
+
+    @pl.when(d == 1)
+    def _():
+        pl.semaphore_signal(barrier, inc=1, device_id=mate, device_id_type=MESH)
+
     for c in range(2):
         pltpu.make_async_copy(tok_hbm.at[c], g.at[c, me], own_sem.at[c]).start()
-    barrier = pltpu.get_barrier_semaphore()
-    for k in range(1, n):
-        pl.semaphore_signal(barrier, inc=1, device_id={COL: wrap(x + k)}, device_id_type=MESH)
-        pl.semaphore_signal(barrier, inc=1, device_id={ROW: wrap(y + k)}, device_id_type=MESH)
-    pl.semaphore_signal(barrier, inc=1, device_id=mate, device_id_type=MESH)
+    taken = ((mb_hbm, mb), (bl_hbm, bl), (cot_hbm, cot))
+    given = ((hidden, hidden_hbm), (igrad, igrad_hbm), (dgrad, dgrad_hbm), (ugrad, ugrad_hbm))
+
+    def take(k):
+        return pltpu.make_async_copy(*taken[k], in_sem.at[k])
+
+    def give(k):
+        return pltpu.make_async_copy(*given[k], out_sem.at[k])
+
+    for k in range(3):
+        take(k).start()
 
     def ad_local(k):
         hbm, vm = ((ain_hbm, ain), (aout_hbm, aout))[k]
@@ -184,7 +208,12 @@
         w_local(q).start()
     for c in range(2):
         landed(g.at[c, me], own_sem.at[c])
-    pl.semaphore_wait(barrier, 2 * (n - 1) + 1)
+    pl.semaphore_wait(barrier, 4 + 1 - d)
+
+    @pl.when(d == 0)
+    def _():
+        pl.semaphore_signal(here, inc=1, device_id=mate, device_id_type=MESH)
+
 
     def minor_offset(j):
         back = lax.div(j + 1, 2)
@@ -275,7 +304,7 @@
 
     def rs1_add_send(c, e, i, s):
         t = rs1_chunk(c, e, i, s)
-        p[c, t] = encode(decode(p[c, t]) + decode(rb[c, e, i, s - 1]))
+        put(p, (c, t), get(p, (c, t)) + get(rb, (c, e, i, s - 1)))
         rs1_copy(c, e, i, s).start()
 
     def rs2_copy(c, i, right):
@@ -285,9 +314,9 @@
 
     def rs1_done(c, i):
         t = chunk(c, major_at[c], wrap(minor_at[c] + dest_offset(i)))
-        total = decode(p[c, t])
+        total = get(p, (c, t))
         for e in range(2):
-            total = total + decode(rb[c, e, i, hops(e, i) - 1])
+            total = total + get(rb, (c, e, i, hops(e, i) - 1))
         return t, total
 
     def rs2_step(i):
@@ -296,13 +325,13 @@
             @pl.when(i < 2)
             def _(c=c):
                 t, total = rs1_done(c, i)
-                p[c, t] = encode(total)
+                put(p, (c, t), total)
 
             @pl.when(jnp.logical_and(i >= 2, i < n - 1))
             def _(c=c):
                 landed(r2.at[c, i - 2], rs2_r.at[c, i - 2])
                 t, total = rs1_done(c, i)
-                p[c, t] = encode(total + decode(r2[c, i - 2]))
+                put(p, (c, t), total + get(r2, (c, i - 2)))
 
             @pl.when(jnp.logical_and(i < n - 1, lax.rem(i, 2) == 0))
             def _(c=c):
@@ -318,7 +347,7 @@
                 total = total + adt[c]
                 for k in (n - 3, n - 2):
                     landed(r2.at[c, k], rs2_r.at[c, k])
-                    total = total + decode(r2[c, k])
+                    total = total + get(r2, (c, k))
                 igrad[c] = total.astype(BF16)
 
     def rs_tick(tick):
@@ -388,17 +417,36 @@
             both = jnp.concatenate([into, back], axis=1)
             each = BLOCK // tall
             part[pl.ds(b * each, each)] = both.reshape(each, tall, 2 * rank)
-        xbuf[x] = part[x]
-
-    def x_copy(k):
-        to = wrap(x + k)
-        return remote(part.at[to], xbuf.at[x], xs.at[k], xr.at[k], {COL: to})
-
-    def y_copy(k):
-        return remote(ybuf.at[y], ybuf.at[y], ys.at[k], yr.at[k], {ROW: wrap(y + k)})
-
-    def z_copy(k):
-        return remote(low.at[x], low.at[x], zs.at[k], zr.at[k], {COL: wrap(x + k)})
+
+    def x_copy(e, s):
+        way = 1 - 2 * e
+        piece = wrap(x + way * (half - e - s))
+        to = {COL: wrap(x + way)}
+        return remote(part.at[piece], xbuf.at[e, s], xs.at[e, s], xr.at[e, s], to)
+
+    def x_step(s):
+        for e in range(2):
+            if 1 <= s <= half - e:
+                piece = wrap(x + (1 - 2 * e) * (half - e - s))
+                landed(xbuf.at[e, s - 1], xr.at[e, s - 1])
+                part[piece] = part[piece] + xbuf[e, s - 1]
+            if s < half - e:
+                x_copy(e, s).start()
+
+    def round_copy(buf, at, axis, ss, rs, e, s):
+        src = wrap(at - (1 - 2 * e) * s)
+        to = {axis: wrap(at + 1 - 2 * e)}
+        return remote(buf.at[src], buf.at[src], ss.at[e, s], rs.at[e, s], to)
+
+    def round_step(ring, s):
+        buf, at, axis, ss, rs = ring
+        for e in range(2):
+            if 1 <= s <= half - e:
+                landed(buf.at[wrap(at - (1 - 2 * e) * s)], rs.at[e, s - 1])
+            if s < half - e:
+                round_copy(*ring, e, s).start()
+
+    y_ring, z_ring = (ybuf, y, ROW, ys, yr), (low, x, COL, zs, zr)
 
     def total_of(ref):
         total = ref[0]
@@ -406,15 +454,17 @@
             total = total + ref[k]
         return total
 
-    def x_done():
-        for k in range(1, n):
-            landed(xbuf.at[wrap(x - k)], xr.at[k])
-        ybuf[y] = total_of(xbuf)
-
-    def y_done():
-        for k in range(1, n):
-            landed(ybuf.at[wrap(y - k)], yr.at[k])
-        low[x] = total_of(ybuf).astype(BF16)
+    def low_step(k):
+        if k <= half:
+            x_step(k)
+        if k == half:
+            ybuf[y] = part[x]
+        if half <= k <= 2 * half:
+            round_step(y_ring, k - half)
+        if k == 2 * half:
+            low[x] = total_of(ybuf).astype(BF16)
+        if 2 * half <= k:
+            round_step(z_ring, k - 2 * half)
 
     def low_of(b):
         each = n // 2
@@ -425,9 +475,7 @@
         src, dst = ((usend, urecv), (dsend, drecv))[k]
         return remote(src, dst, gx_s.at[k], gx_r.at[k], mate)
 
-    def z_done():
-        for k in range(1, n):
-            landed(low.at[wrap(x - k)], zr.at[k])
+    def grads_start():
         ups, downs = [], []
         for b in range(2):
             into, back = low_of(b)
@@ -444,7 +492,7 @@
         for b in range(2):
             into, back = low_of(b)
             turned = jnp.transpose(into.astype(F32)).astype(BF16)
-            acc[:, b * BLOCK : (b + 1) * BLOCK] = SCALE * dot(cout[b], turned, TN)
+            acc[:, b * BLOCK : (b + 1) * BLOCK] += SCALE * dot(cout[b], turned, TN)
             adt[b] = SCALE * dot(back, cin[b], NN)
 
     def grads_done():
@@ -453,12 +501,14 @@
         for q in range(owned):
             ugrad[q] = ugrad[q] + urecv[q]
             dgrad[q] = dgrad[q] + drecv[q]
+        give(2).start()
+        give(3).start()
 
     def back_chunk(k):
         t = lax.rem(d * own_chunks + k, chunks)
         out = dot(masked[...], w_chunk(t), NN)
         for b in range(2):
-            p[b, t] = encode(out[b * BLOCK : (b + 1) * BLOCK])
+            put(p, (b, t), out[b * BLOCK : (b + 1) * BLOCK])
 
     def front_chunk(t):
         rows_in = jnp.concatenate([g[0, t], g[1, t]], axis=0)
@@ -468,6 +518,7 @@
         for b in range(2):
             cols = acc[:, b * BLOCK : (b + 1) * BLOCK]
             hidden[:, b * BLOCK : (b + 1) * BLOCK] = (cols * live(b, cols.shape, 1)).astype(BF16)
+        give(0).start()
 
     def some(body, first, last):
         lax.fori_loop(first, last, lambda k, z: (body(k), z)[1], 0)
@@ -476,7 +527,7 @@
     last = rs_from + ticks - 1
     back_from, back_ticks = early, rs_from - early
     back_each = -(-chunks // back_ticks)
-    front_from, front_ticks = ticks, last - 1 - ticks
+    front_from, front_ticks = ticks, half + 1
     front_each = -(-chunks // front_ticks)
 
     def every_tick(tick, carry):
@@ -488,41 +539,46 @@
         def _():
             rs_tick(tick - rs_from)
 
-        @pl.when(tick == 0)
-        def _():
+        @pl.when(tick == early - 1)
+        def _():
+            @pl.when(d == 1)
+            def _():
+                pl.semaphore_wait(here, 1)
+
             for k in range(2):
                 ad_remote(k).start()
             for q in range(pieces):
                 w_remote(q).start()
+            for k in range(3):
+                take(k).wait()
             mask_step()
+            acc[...] = jnp.zeros_like(acc)
+
+        @pl.when(tick == low_from)
+        def _():
             low_rank_start()
-            for k in range(1, n):
-                x_copy(k).start()
-
-        @pl.when(tick == early)
-        def _():
-            x_done()
-            for k in range(1, n):
-                y_copy(k).start()
             for q in range(pieces):
                 w_local(q).wait()
 
+        for k in range(3 * half + 1):
+
+            @pl.when(tick == low_from + k)
+            def _(k=k):
+                low_step(k)
+
         @pl.when(tick == middle)
         def _():
-            y_done()
-            for k in range(1, n):
-                z_copy(k).start()
             for q in range(pieces):
                 landed(w_piece(1 - d, q), wx_r.at[q])
 
-        @pl.when(tick == late)
-        def _():
-            z_done()
+        @pl.when(tick == low_to)
+        def _():
+            grads_start()
             for k in range(2):
                 g_copy(k).start()
             terms_step()
 
-        @pl.when(tick == rs_from + 1)
+        @pl.when(tick == low_to + 1)
         def _():
             grads_done()
 
@@ -543,16 +599,19 @@
         return carry
 
     lax.fori_loop(0, last + 1, every_tick, 0)
+
+    give(1).start()
 
     for k in range(2):
         ad_remote(k).wait_send()
         g_copy(k).wait_send()
     for q in range(pieces):
         w_remote(q).wait_send()
-    for k in range(1, n):
-        x_copy(k).wait_send()
-        y_copy(k).wait_send()
-        z_copy(k).wait_send()
+    for e in range(2):
+        for s in range(half - e):
+            x_copy(e, s).wait_send()
+            round_copy(*y_ring, e, s).wait_send()
+            round_copy(*z_ring, e, s).wait_send()
 
     def sent(src, sem):
         pltpu.make_async_copy(src, src, sem).wait()
@@ -582,6 +641,8 @@
         return carry
 
     lax.fori_loop(0, n, drain, 0)
+    for k in range(4):
+        give(k).wait()
 
 
 def hand_over(*refs):
@@ -598,11 +659,9 @@
     half = n // 2
     tall = token_rows // n
     chunks = n * n
-    vmem, anywhere, smem = (
-        pl.BlockSpec(memory_space=s) for s in (pltpu.VMEM, pl.ANY, pltpu.SMEM)
-    )
+    vmem, anywhere = (pl.BlockSpec(memory_space=s) for s in (pltpu.VMEM, pl.ANY))
     pieces = 4
-    coded = BLOCK * width // (2 * LANES) + SUBLANES
+    coded = BLOCK * width // (2 * LANES) + 1
     dma = lambda *shape: pltpu.SemaphoreType.DMA(shape)
     both_ways = (2, 2, n, half)
     out = pl.pallas_call(
@@ -613,9 +672,16 @@
             jax.ShapeDtypeStruct((owned, rank, width), F32),
             jax.ShapeDtypeStruct((owned, rank, hidden_width), F32),
         ),
-        in_specs=[smem, smem, anywhere, anywhere, anywhere, anywhere, vmem],
-        out_specs=(vmem,) * 4,
+        in_specs=[anywhere] * 7,
+        out_specs=(anywhere,) * 4,
         scratch_shapes=[
+            pltpu.SMEM(member_blocks.shape, jnp.int32),
+            pltpu.SMEM(block_live.shape, jnp.int32),
+            pltpu.VMEM((hidden_width, token_rows), BF16),
+            pltpu.VMEM((hidden_width, token_rows), BF16),
+            pltpu.VMEM((blocks, BLOCK, width), BF16),
+            pltpu.VMEM((owned, rank, width), F32),
+            pltpu.VMEM((owned, rank, hidden_width), F32),
             pltpu.VMEM((blocks, chunks, BLOCK, width), BF16),
             pltpu.VMEM((hidden_width, chunks * width), BF16),
             pltpu.VMEM((blocks, chunks, coded, LANES), jnp.int32),
@@ -629,7 +695,7 @@
             pltpu.VMEM((blocks, rank, width), BF16),
             pltpu.VMEM((blocks, rank, hidden_width), BF16),
             pltpu.VMEM((n, tall, 2 * rank), F32),
-            pltpu.VMEM((n, tall, 2 * rank), F32),
+            pltpu.VMEM((2, half, tall, 2 * rank), F32),
             pltpu.VMEM((n, tall, 2 * rank), F32),
             pltpu.VMEM((n, tall, 2 * rank), BF16),
             pltpu.VMEM((owned, rank, hidden_width), F32),
@@ -651,14 +717,17 @@
             dma(2),
             dma(2),
             dma(2),
-            dma(n),
-            dma(n),
-            dma(n),
-            dma(n),
-            dma(n),
-            dma(n),
+            dma(2, half),
+            dma(2, half),
+            dma(2, half),
+            dma(2, half),
+            dma(2, half),
+            dma(2, half),
             dma(2),
             dma(2),
+            dma(3),
+            dma(4),
+            pltpu.SemaphoreType.REGULAR,
         ],
         compiler_params=pltpu.CompilerParams(
             collective_id=0, has_side_effects=True, vmem_limit_bytes=62 * 2**20

time: 138 us -> 133 us (0.964)
  Pallas kernels: 137 us -> 132 us
    pallas_call x1, Pallas kernels: 135 us -> 130 us  [local(): pl.pallas_call(functools.partial(kernel, n), out_shape=(jax.ShapeDtypeStr...]
where the time goes in v3:
time: 133 us
  Pallas kernels  132 us (99%)
    pallas_call x1, Pallas kernels, local(): pl.pallas_call(functools.partial(kernel, n), out_shape=(jax.ShapeDtypeStr...  130 us

profile of v3, /device:TPU:514, one launch (start us, length us, event | category | flops | bytes accessed | tf_op | source)
XLA Modules:
  0.0 132.7 jit_solution(15106804966766415453)
XLA Ops:
  0.6 130.0 %step.1 = (bf16[416,256]{1,0:T(8,128)(2,1)}, bf16[2,128,256]{2,1,0:T(8,128)(2,1)}, f32[2,64,256]{2,1,0:T(8,128)}, f32[2,64,416]{2,1,0:T(8,128)}) custom-call(s32[4]{0:T(128)} %mb_hbm.1, s32[2]{0:T(128)} %bl_hbm.1, bf16[2,128,256]{2,1,0:T(8,128)(2,1)} %bitcast.9, bf16[416,8192]{1,0:T(8,128)(2,1)} %bitcast.7, bf16[2,64,256]{2,1,0:T(8,128)(2,1)} %bitcast.10, ...), custom_call_target="tpu_custom_call" | custom-call | tf_op jit(solution)/shard_map/step/pallas_call | solution.py:667
  130.7 2.1 %hand_over.1 = (bf16[416,256]{1,0:T(8,128)(2,1)}, bf16[2,128,256]{2,1,0:T(8,128)(2,1)}, f32[2,64,256]{2,1,0:T(8,128)}, f32[2,64,416]{2,1,0:T(8,128)}) custom-call(bf16[416,256]{1,0:T(8,128)(2,1)} %get-tuple-element.12.refs_0_, bf16[2,128,256]{2,1,0:T(8,128)(2,1)} %get-tuple-element.13.refs_1_, f32[2,64,256]{2,1,0:T(8,128)} %get-tuple-element.14.refs_2_, ...), custom_call_target="tpu_custom_call" | custom-call | tf_op jit(solution)/shard_map/hand_over/pallas_call | solution.py:745

commit v4 on v3

--- a/solution.py
+++ b/solution.py
@@ -96,14 +96,10 @@
     dsend,
     urecv,
     drecv,
-    ag1_s,
-    ag1_r,
-    ag2_s,
-    ag2_r,
-    rs1_s,
-    rs1_r,
-    rs2_s,
-    rs2_r,
+    ag_s,
+    rs_s,
+    flow_r,
+    turn_r,
     own_sem,
     w_sem,
     wx_s,
@@ -111,12 +107,9 @@
     ad_sem,
     adx_s,
     adx_r,
-    xs,
-    xr,
-    ys,
-    yr,
-    zs,
-    zr,
+    low_s,
+    xz_r,
+    y_r,
     gx_s,
     gx_r,
     in_sem,
@@ -124,7 +117,8 @@
     here,
 ):
     half = n // 2
-    ticks = n + half
+    ticks = n - 1 + half
+    cycle, shift = (5, 3) if n >= 8 else (2 * n, n)
     early, middle = n // 4, n // 2
     low_from = early
     low_to = low_from + 3 * half
@@ -137,8 +131,6 @@
     width = g.shape[3]
     own_depth = w_hbm.shape[1]
     own_chunks = own_depth // width
-    pieces = w_sem.shape[0]
-    piece = own_depth // pieces
     rank = ain.shape[1]
     minor_axis, major_axis = (COL, ROW), (ROW, COL)
     minor_at, major_at = (x, y), (y, x)
@@ -166,8 +158,8 @@
     def _():
         pl.semaphore_signal(barrier, inc=1, device_id=mate, device_id_type=MESH)
 
-    for c in range(2):
-        pltpu.make_async_copy(tok_hbm.at[c], g.at[c, me], own_sem.at[c]).start()
+    own = pltpu.make_async_copy(tok_hbm, g.at[:, me], own_sem)
+    own.start()
     taken = ((mb_hbm, mb), (bl_hbm, bl), (cot_hbm, cot))
     given = ((hidden, hidden_hbm), (igrad, igrad_hbm), (dgrad, dgrad_hbm), (ugrad, ugrad_hbm))
 
@@ -188,26 +180,19 @@
         hbm, vm = ((ain_hbm, ain), (aout_hbm, aout))[k]
         return remote(hbm, vm.at[pl.ds(d * owned, owned)], adx_s.at[k], adx_r.at[k], mate)
 
-    def w_piece(core, q):
-        return w.at[:, pl.ds(pl.multiple_of(core * own_depth + q * piece, LANES), piece)]
-
-    def w_local(q):
-        src = w_hbm.at[:, pl.ds(q * piece, piece)]
-        return pltpu.make_async_copy(src, w_piece(d, q), w_sem.at[q])
-
-    def w_remote(q):
-        src = w_hbm.at[:, pl.ds(q * piece, piece)]
-        return remote(src, w_piece(d, q), wx_s.at[q], wx_r.at[q], mate)
+    def w_half(core):
+        return w.at[:, pl.ds(pl.multiple_of(core * own_depth, LANES), own_depth)]
+
+    w_local = pltpu.make_async_copy(w_hbm, w_half(d), w_sem)
+    w_remote = remote(w_hbm, w_half(d), wx_s, wx_r, mate)
 
     def w_chunk(t):
         return w[:, pl.ds(pl.multiple_of(t * width, LANES), width)]
 
     for k in range(2):
         ad_local(k).start()
-    for q in range(pieces):
-        w_local(q).start()
-    for c in range(2):
-        landed(g.at[c, me], own_sem.at[c])
+    w_local.start()
+    own.wait()
     pl.semaphore_wait(barrier, 4 + 1 - d)
 
     @pl.when(d == 0)
@@ -223,7 +208,7 @@
         src = chunk(c, major_at[c], wrap(minor_at[c] + minor_offset(j)))
         lands = jnp.where(j == 0, 1 if right else 2, j + 2)
         to = {minor_axis[c]: wrap(minor_at[c] + (1 if right else -1))}
-        return remote(g.at[c, src], g.at[c, src], ag1_s.at[c, lands], ag1_r.at[c, lands], to)
+        return remote(g.at[c, src], g.at[c, src], ag_s.at[c], turn_r.at[c, lands], to)
 
     def ag1_step(j):
         for c in range(2):
@@ -231,7 +216,7 @@
 
             @pl.when(j >= 1)
             def _(c=c, src=src):
-                landed(g.at[c, src], ag1_r.at[c, j])
+                landed(g.at[c, src], turn_r.at[c, j])
 
             @pl.when(jnp.logical_or(j == 0, jnp.logical_and(lax.rem(j, 2) == 1, j + 2 < n)))
             def _(c=c):
@@ -245,28 +230,27 @@
         way = 1 - 2 * e
         t = chunk(c, wrap(major_at[c] - way * s), wrap(minor_at[c] + minor_offset(j)))
         to = {major_axis[c]: wrap(major_at[c] + way)}
-        return remote(g.at[c, t], g.at[c, t], ag2_s.at[c, e, j, s], ag2_r.at[c, e, j, s], to)
+        return remote(g.at[c, t], g.at[c, t], ag_s.at[c], flow_r.at[c, e, lax.rem(j, cycle), s], to)
 
     def ag2_landed(c, e, j, s):
         t = chunk(c, wrap(major_at[c] - (1 - 2 * e) * s), wrap(minor_at[c] + minor_offset(j)))
-        landed(g.at[c, t], ag2_r.at[c, e, j, s - 1])
+        landed(g.at[c, t], flow_r.at[c, e, lax.rem(j, cycle), s - 1])
 
     def is_long(e, j):
         return lax.rem(j, 2) == e
 
-    def live_stream(j):
-        return jnp.logical_and(j >= 0, j < n)
+    def streams(at, first, body):
+        j = at + jnp.where(at > first, 1, 0)
+
+        @pl.when(jnp.logical_and(at >= 0, at < n - 1))
+        def _():
+            lax.fori_loop(j, j + 1 + jnp.where(at == first, 1, 0), lambda k, z: (body(k), z)[1], 0)
 
     def ag_tick(tick):
-        @pl.when(tick < n)
-        def _():
-            ag1_step(tick)
-
+        streams(tick, 1, ag1_step)
         for s in range(half + 1):
-            j = tick - s
-
-            @pl.when(live_stream(j))
-            def _(j=j, s=s):
+
+            def hop(j, s=s):
                 for c in range(2):
                     for e in range(2):
                         if s < half:
@@ -285,6 +269,8 @@
                             def _(c=c, e=e):
                                 ag2_landed(c, e, j, s)
 
+            streams(tick - s, 1, hop)
+
     def dest_offset(i):
         ahead = lax.div(n - i, 2)
         back = lax.div(n - 1 - i, 2)
@@ -297,10 +283,16 @@
         far = (1 - 2 * e) * (hops(e, i) - s)
         return chunk(c, wrap(major_at[c] + far), wrap(minor_at[c] + dest_offset(i)))
 
+    def rs1_sem(c, e, i, s):
+        return flow_r.at[c, e, lax.rem(i + shift, cycle), s]
+
+    def rs1_landed(c, e, i, s):
+        landed(rb.at[c, e, i, s], rs1_sem(c, e, i, s))
+
     def rs1_copy(c, e, i, s):
         t = rs1_chunk(c, e, i, s)
         to = {major_axis[c]: wrap(major_at[c] + 1 - 2 * e)}
-        return remote(p.at[c, t], rb.at[c, e, i, s], rs1_s.at[c, e, i, s], rs1_r.at[c, e, i, s], to)
+        return remote(p.at[c, t], rb.at[c, e, i, s], rs_s.at[c], rs1_sem(c, e, i, s), to)
 
     def rs1_add_send(c, e, i, s):
         t = rs1_chunk(c, e, i, s)
@@ -310,7 +302,7 @@
     def rs2_copy(c, i, right):
         t = chunk(c, major_at[c], wrap(minor_at[c] + dest_offset(i)))
         to = {minor_axis[c]: wrap(minor_at[c] + (1 if right else -1))}
-        return remote(p.at[c, t], r2.at[c, i], rs2_s.at[c, i], rs2_r.at[c, i], to)
+        return remote(p.at[c, t], r2.at[c, i], rs_s.at[c], turn_r.at[c, i], to)
 
     def rs1_done(c, i):
         t = chunk(c, major_at[c], wrap(minor_at[c] + dest_offset(i)))
@@ -329,7 +321,7 @@
 
             @pl.when(jnp.logical_and(i >= 2, i < n - 1))
             def _(c=c):
-                landed(r2.at[c, i - 2], rs2_r.at[c, i - 2])
+                landed(r2.at[c, i - 2], turn_r.at[c, i - 2])
                 t, total = rs1_done(c, i)
                 put(p, (c, t), total + get(r2, (c, i - 2)))
 
@@ -346,25 +338,23 @@
                 t, total = rs1_done(c, i)
                 total = total + adt[c]
                 for k in (n - 3, n - 2):
-                    landed(r2.at[c, k], rs2_r.at[c, k])
+                    landed(r2.at[c, k], turn_r.at[c, k])
                     total = total + get(r2, (c, k))
                 igrad[c] = total.astype(BF16)
 
     def rs_tick(tick):
         for s in range(half + 1):
-            i = tick - s
-
-            @pl.when(live_stream(i))
-            def _(i=i, s=s):
+
+            def hop(i, s=s):
                 for c in range(2):
                     for e in range(2):
                         if s == 0:
                             rs1_copy(c, e, i, s).start()
                         elif s < half - 1:
-                            landed(rb.at[c, e, i, s - 1], rs1_r.at[c, e, i, s - 1])
+                            rs1_landed(c, e, i, s - 1)
                             rs1_add_send(c, e, i, s)
                         elif s == half - 1:
-                            landed(rb.at[c, e, i, s - 1], rs1_r.at[c, e, i, s - 1])
+                            rs1_landed(c, e, i, s - 1)
 
                             @pl.when(is_long(e, i))
                             def _(c=c, e=e):
@@ -373,10 +363,12 @@
 
                             @pl.when(is_long(e, i))
                             def _(c=c, e=e):
-                                landed(rb.at[c, e, i, s - 1], rs1_r.at[c, e, i, s - 1])
+                                rs1_landed(c, e, i, s - 1)
 
                 if s == half:
                     rs2_step(i)
+
+            streams(tick - s, n - 3, hop)
 
     def member_of(b):
         end, count = jnp.int32(0), jnp.int32(0)
@@ -422,13 +414,13 @@
         way = 1 - 2 * e
         piece = wrap(x + way * (half - e - s))
         to = {COL: wrap(x + way)}
-        return remote(part.at[piece], xbuf.at[e, s], xs.at[e, s], xr.at[e, s], to)
+        return remote(part.at[piece], xbuf.at[e, s], low_s.at[0], xz_r.at[e, s], to)
 
     def x_step(s):
         for e in range(2):
             if 1 <= s <= half - e:
                 piece = wrap(x + (1 - 2 * e) * (half - e - s))
-                landed(xbuf.at[e, s - 1], xr.at[e, s - 1])
+                landed(xbuf.at[e, s - 1], xz_r.at[e, s - 1])
                 part[piece] = part[piece] + xbuf[e, s - 1]
             if s < half - e:
                 x_copy(e, s).start()
@@ -436,7 +428,7 @@
     def round_copy(buf, at, axis, ss, rs, e, s):
         src = wrap(at - (1 - 2 * e) * s)
         to = {axis: wrap(at + 1 - 2 * e)}
-        return remote(buf.at[src], buf.at[src], ss.at[e, s], rs.at[e, s], to)
+        return remote(buf.at[src], buf.at[src], ss, rs.at[e, s], to)
 
     def round_step(ring, s):
         buf, at, axis, ss, rs = ring
@@ -446,7 +438,7 @@
             if s < half - e:
                 round_copy(*ring, e, s).start()
 
-    y_ring, z_ring = (ybuf, y, ROW, ys, yr), (low, x, COL, zs, zr)
+    y_ring, z_ring = (ybuf, y, ROW, low_s.at[1], y_r), (low, x, COL, low_s.at[2], xz_r)
 
     def total_of(ref):
         total = ref[0]
@@ -523,8 +515,8 @@
     def some(body, first, last):
         lax.fori_loop(first, last, lambda k, z: (body(k), z)[1], 0)
 
-    rs_from = n
-    last = rs_from + ticks - 1
+    rs_from = n - 1 if n >= 8 else n + 1
+    last = max(rs_from + ticks - 1, low_to + 2)
     back_from, back_ticks = early, rs_from - early
     back_each = -(-chunks // back_ticks)
     front_from, front_ticks = ticks, half + 1
@@ -547,8 +539,7 @@
 
             for k in range(2):
                 ad_remote(k).start()
-            for q in range(pieces):
-                w_remote(q).start()
+            w_remote.start()
             for k in range(3):
                 take(k).wait()
             mask_step()
@@ -557,8 +548,7 @@
         @pl.when(tick == low_from)
         def _():
             low_rank_start()
-            for q in range(pieces):
-                w_local(q).wait()
+            w_local.wait()
 
         for k in range(3 * half + 1):
 
@@ -568,8 +558,7 @@
 
         @pl.when(tick == middle)
         def _():
-            for q in range(pieces):
-                landed(w_piece(1 - d, q), wx_r.at[q])
+            landed(w_half(1 - d), wx_r)
 
         @pl.when(tick == low_to)
         def _():
@@ -578,7 +567,7 @@
                 g_copy(k).start()
             terms_step()
 
-        @pl.when(tick == low_to + 1)
+        @pl.when(tick == low_to + 2)
         def _():
             grads_done()
 
@@ -605,42 +594,16 @@
     for k in range(2):
         ad_remote(k).wait_send()
         g_copy(k).wait_send()
-    for q in range(pieces):
-        w_remote(q).wait_send()
-    for e in range(2):
-        for s in range(half - e):
-            x_copy(e, s).wait_send()
-            round_copy(*y_ring, e, s).wait_send()
-            round_copy(*z_ring, e, s).wait_send()
+    w_remote.wait_send()
 
     def sent(src, sem):
         pltpu.make_async_copy(src, src, sem).wait()
 
-    def drain(j, carry):
-        @pl.when(j >= 1)
-        def _():
-            for c in range(2):
-                sent(g.at[c, 0], ag1_s.at[c, j])
-
-        @pl.when(j < n - 1)
-        def _():
-            for c in range(2):
-                sent(p.at[c, 0], rs2_s.at[c, j])
-
-        for c in range(2):
-            for e in range(2):
-                for s in range(half - 1):
-                    sent(g.at[c, 0], ag2_s.at[c, e, j, s])
-                    sent(p.at[c, 0], rs1_s.at[c, e, j, s])
-
-                @pl.when(is_long(e, j))
-                def _(c=c, e=e):
-                    sent(g.at[c, 0], ag2_s.at[c, e, j, half - 1])
-                    sent(p.at[c, 0], rs1_s.at[c, e, j, half - 1])
-
-        return carry
-
-    lax.fori_loop(0, n, drain, 0)
+    for k, buf in enumerate((part, ybuf, low)):
+        sent(buf.at[pl.ds(0, n - 1)], low_s.at[k])
+    for c in range(2):
+        sent(g.at[c, pl.ds(0, chunks - 1)], ag_s.at[c])
+        sent(p.at[c, pl.ds(0, chunks - 1)], rs_s.at[c])
     for k in range(4):
         give(k).wait()
 
@@ -660,7 +623,6 @@
     tall = token_rows // n
     chunks = n * n
     vmem, anywhere = (pl.BlockSpec(memory_space=s) for s in (pltpu.VMEM, pl.ANY))
-    pieces = 4
     coded = BLOCK * width // (2 * LANES) + 1
     dma = lambda *shape: pltpu.SemaphoreType.DMA(shape)
     both_ways = (2, 2, n, half)
@@ -702,25 +664,18 @@
             pltpu.VMEM((owned, rank, width), F32),
             pltpu.VMEM((owned, rank, hidden_width), F32),
             pltpu.VMEM((owned, rank, width), F32),
+            dma(2),
+            dma(2),
+            dma(2, 2, 5 if n >= 8 else 2 * n, half),
             dma(2, n),
-            dma(2, n),
-            dma(*both_ways),
-            dma(*both_ways),
-            dma(*both_ways),
-            dma(*both_ways),
-            dma(2, n),
-            dma(2, n),
-            dma(2),
-            dma(pieces),
-            dma(pieces),
-            dma(pieces),
+            pltpu.SemaphoreType.DMA,
+            pltpu.SemaphoreType.DMA,
+            pltpu.SemaphoreType.DMA,
+            pltpu.SemaphoreType.DMA,
             dma(2),
             dma(2),
             dma(2),
-            dma(2, half),
-            dma(2, half),
-            dma(2, half),
-            dma(2, half),
+            dma(3),
             dma(2, half),
             dma(2, half),
             dma(2),

time: 133 us -> 124 us (0.932)
  Pallas kernels: 132 us -> 124 us
    pallas_call x1, Pallas kernels: 130 us -> 122 us  [local(): pl.pallas_call(functools.partial(kernel, n), out_shape=(jax.ShapeDtypeStr...]
where the time goes in v4:
time: 124 us
  Pallas kernels  124 us (100%)
    pallas_call x1, Pallas kernels, local(): pl.pallas_call(functools.partial(kernel, n), out_shape=(jax.ShapeDtypeStr...  122 us

profile of v4, /device:TPU:514, one launch (start us, length us, event | category | flops | bytes accessed | tf_op | source)
XLA Modules:
  0.0 124.3 jit_solution(11013722072374791460)
XLA Ops:
  0.6 121.6 %step.1 = (bf16[416,256]{1,0:T(8,128)(2,1)}, bf16[2,128,256]{2,1,0:T(8,128)(2,1)}, f32[2,64,256]{2,1,0:T(8,128)}, f32[2,64,416]{2,1,0:T(8,128)}) custom-call(s32[4]{0:T(128)} %mb_hbm.1, s32[2]{0:T(128)} %bl_hbm.1, bf16[2,128,256]{2,1,0:T(8,128)(2,1)} %bitcast.9, bf16[416,8192]{1,0:T(8,128)(2,1)} %bitcast.7, bf16[2,64,256]{2,1,0:T(8,128)(2,1)} %bitcast.10, ...), custom_call_target="tpu_custom_call" | custom-call | tf_op jit(solution)/shard_map/step/pallas_call | solution.py:629
  122.2 2.1 %hand_over.1 = (bf16[416,256]{1,0:T(8,128)(2,1)}, bf16[2,128,256]{2,1,0:T(8,128)(2,1)}, f32[2,64,256]{2,1,0:T(8,128)}, f32[2,64,416]{2,1,0:T(8,128)}) custom-call(bf16[416,256]{1,0:T(8,128)(2,1)} %get-tuple-element.12.refs_0_, bf16[2,128,256]{2,1,0:T(8,128)(2,1)} %get-tuple-element.13.refs_1_, f32[2,64,256]{2,1,0:T(8,128)} %get-tuple-element.14.refs_2_, ...), custom_call_target="tpu_custom_call" | custom-call | tf_op jit(solution)/shard_map/hand_over/pallas_call | solution.py:700

commit v5 on v4

--- a/solution.py
+++ b/solution.py
@@ -65,17 +65,13 @@
     ain_hbm,
     aout_hbm,
     cot_hbm,
-    hidden_hbm,
-    igrad_hbm,
-    dgrad_hbm,
-    ugrad_hbm,
-    mb,
-    bl,
-    cot,
     hidden,
     igrad,
     dgrad,
     ugrad,
+    mb,
+    bl,
+    cot,
     g,
     w,
     p,
@@ -113,7 +109,6 @@
     gx_s,
     gx_r,
     in_sem,
-    out_sem,
     here,
 ):
     half = n // 2
@@ -126,6 +121,7 @@
     mate = {CORE: 1 - d}
     me = y * n + x
     chunks = n * n
+    group = 4
     members = ain.shape[0]
     owned = members // 2
     width = g.shape[3]
@@ -161,13 +157,9 @@
     own = pltpu.make_async_copy(tok_hbm, g.at[:, me], own_sem)
     own.start()
     taken = ((mb_hbm, mb), (bl_hbm, bl), (cot_hbm, cot))
-    given = ((hidden, hidden_hbm), (igrad, igrad_hbm), (dgrad, dgrad_hbm), (ugrad, ugrad_hbm))
 
     def take(k):
         return pltpu.make_async_copy(*taken[k], in_sem.at[k])
-
-    def give(k):
-        return pltpu.make_async_copy(*given[k], out_sem.at[k])
 
     for k in range(3):
         take(k).start()
@@ -493,8 +485,6 @@
         for q in range(owned):
             ugrad[q] = ugrad[q] + urecv[q]
             dgrad[q] = dgrad[q] + drecv[q]
-        give(2).start()
-        give(3).start()
 
     def back_chunk(k):
         t = lax.rem(d * own_chunks + k, chunks)
@@ -502,15 +492,18 @@
         for b in range(2):
             put(p, (b, t), out[b * BLOCK : (b + 1) * BLOCK])
 
-    def front_chunk(t):
-        rows_in = jnp.concatenate([g[0, t], g[1, t]], axis=0)
-        acc[...] += dot(w_chunk(t), rows_in, NT)
+    def front_group(k):
+        first = k * group
+        rows_in = jnp.concatenate(
+            [jnp.concatenate([g[0, first + i], g[1, first + i]], axis=0) for i in range(group)], axis=1
+        )
+        at = pl.multiple_of(first * width, LANES)
+        acc[...] += dot(w[:, pl.ds(at, group * width)], rows_in, NT)
 
     def hidden_step():
         for b in range(2):
             cols = acc[:, b * BLOCK : (b + 1) * BLOCK]
             hidden[:, b * BLOCK : (b + 1) * BLOCK] = (cols * live(b, cols.shape, 1)).astype(BF16)
-        give(0).start()
 
     def some(body, first, last):
         lax.fori_loop(first, last, lambda k, z: (body(k), z)[1], 0)
@@ -519,8 +512,8 @@
     last = max(rs_from + ticks - 1, low_to + 2)
     back_from, back_ticks = early, rs_from - early
     back_each = -(-chunks // back_ticks)
-    front_from, front_ticks = ticks, half + 1
-    front_each = -(-chunks // front_ticks)
+    front_from, front_ticks = ticks, 3
+    front_each = -(-(chunks // group) // front_ticks)
 
     def every_tick(tick, carry):
         @pl.when(tick < ticks)
@@ -579,7 +572,7 @@
         @pl.when(jnp.logical_and(tick >= front_from, tick < front_from + front_ticks))
         def _():
             first = (tick - front_from) * front_each
-            some(front_chunk, first, jnp.minimum(first + front_each, chunks))
+            some(front_group, first, jnp.minimum(first + front_each, chunks // group))
 
         @pl.when(tick == front_from + front_ticks)
         def _():
@@ -589,7 +582,6 @@
 
     lax.fori_loop(0, last + 1, every_tick, 0)
 
-    give(1).start()
 
     for k in range(2):
         ad_remote(k).wait_send()
@@ -604,13 +596,14 @@
     for c in range(2):
         sent(g.at[c, pl.ds(0, chunks - 1)], ag_s.at[c])
         sent(p.at[c, pl.ds(0, chunks - 1)], rs_s.at[c])
-    for k in range(4):
-        give(k).wait()
 
 
 def hand_over(*refs):
-    for src, dst in zip(refs[:4], refs[4:]):
-        dst[...] = src[...]
+    copies = [pltpu.make_async_copy(refs[k], refs[4 + k], refs[8].at[k]) for k in range(4)]
+    for copy in copies:
+        copy.start()
+    for copy in copies:
+        copy.wait()
 
 
 def local(n, tokens, weight, adapter_in, adapter_out, cotangent, member_blocks, block_live):
@@ -622,7 +615,7 @@
     half = n // 2
     tall = token_rows // n
     chunks = n * n
-    vmem, anywhere = (pl.BlockSpec(memory_space=s) for s in (pltpu.VMEM, pl.ANY))
+    vmem, hbm = (pl.BlockSpec(memory_space=s) for s in (pltpu.VMEM, pltpu.HBM))
     coded = BLOCK * width // (2 * LANES) + 1
     dma = lambda *shape: pltpu.SemaphoreType.DMA(shape)
     both_ways = (2, 2, n, half)
@@ -634,16 +627,12 @@
             jax.ShapeDtypeStruct((owned, rank, width), F32),
             jax.ShapeDtypeStruct((owned, rank, hidden_width), F32),
         ),
-        in_specs=[anywhere] * 7,
-        out_specs=(anywhere,) * 4,
+        in_specs=[hbm] * 7,
+        out_specs=(vmem,) * 4,
         scratch_shapes=[
             pltpu.SMEM(member_blocks.shape, jnp.int32),
             pltpu.SMEM(block_live.shape, jnp.int32),
             pltpu.VMEM((hidden_width, token_rows), BF16),
-            pltpu.VMEM((hidden_width, token_rows), BF16),
-            pltpu.VMEM((blocks, BLOCK, width), BF16),
-            pltpu.VMEM((owned, rank, width), F32),
-            pltpu.VMEM((owned, rank, hidden_width), F32),
             pltpu.VMEM((blocks, chunks, BLOCK, width), BF16),
             pltpu.VMEM((hidden_width, chunks * width), BF16),
             pltpu.VMEM((blocks, chunks, coded, LANES), jnp.int32),
@@ -681,27 +670,33 @@
             dma(2),
             dma(2),
             dma(3),
-            dma(4),
             pltpu.SemaphoreType.REGULAR,
         ],
         compiler_params=pltpu.CompilerParams(
-            collective_id=0, has_side_effects=True, vmem_limit_bytes=62 * 2**20
+            collective_id=0, has_side_effects=True, vmem_limit_bytes=47 * 2**20
         ),
         name="step",
     )(
-        member_blocks,
-        block_live,
-        tokens.reshape(blocks, BLOCK, width),
-        weight.T,
-        jnp.swapaxes(adapter_in, 1, 2),
-        adapter_out,
-        cotangent.T,
+        *(
+            pltpu.with_memory_space_constraint(v, pltpu.HBM)
+            for v in (
+                member_blocks,
+                block_live,
+                tokens.reshape(blocks, BLOCK, width),
+                weight.T,
+                jnp.swapaxes(adapter_in, 1, 2),
+                adapter_out,
+                cotangent.T,
+            )
+        )
     )
     out = pl.pallas_call(
         hand_over,
         out_shape=tuple(jax.ShapeDtypeStruct(o.shape, o.dtype) for o in out),
         in_specs=[vmem] * 4,
-        out_specs=(vmem,) * 4,
+        out_specs=(hbm,) * 4,
+        scratch_shapes=[dma(4)],
+        compiler_params=pltpu.CompilerParams(vmem_limit_bytes=4 * 2**20),
         name="hand_over",
     )(*out)
     return (

time: 124 us -> 120 us (0.968)
  Pallas kernels: 124 us -> 120 us
    pallas_call x1, Pallas kernels: 122 us -> 119 us  [local(): pl.pallas_call(functools.partial(kernel, n), out_shape=(jax.ShapeDtypeStr...]
where the time goes in v5:
time: 120 us
  Pallas kernels  120 us (100%)
    pallas_call x1, Pallas kernels, local(): pl.pallas_call(functools.partial(kernel, n), out_shape=(jax.ShapeDtypeStr...  119 us

profile of v5, /device:TPU:514, one launch (start us, length us, event | category | flops | bytes accessed | tf_op | source)
XLA Modules:
  0.0 120.2 jit_solution(16928375888210684874)
XLA Ops:
  0.6 118.7 %step.1 = (bf16[416,256]{1,0:T(8,128)(2,1)S(1)}, bf16[2,128,256]{2,1,0:T(8,128)(2,1)S(1)}, f32[2,64,256]{2,1,0:T(8,128)S(1)}, f32[2,64,416]{2,1,0:T(8,128)S(1)}) custom-call(s32[4]{0:T(128)} %mb_hbm.1, s32[2]{0:T(128)} %bl_hbm.1, bf16[2,128,256]{2,1,0:T(8,128)(2,1)} %bitcast.9, bf16[416,8192]{1,0:T(8,128)(2,1)} %bitcast.7, bf16[2,64,256]{2,1,0:T(8,128)(2,1)} %bitcast.10, ...), custom_call_target="tpu_custom_call" | custom-call | tf_op jit(solution)/shard_map/step/pallas_call | solution.py:622
  119.3 0.9 hand_over.1

commit v6 on v5

--- a/solution.py
+++ b/solution.py
@@ -96,6 +96,7 @@
     rs_s,
     flow_r,
     turn_r,
+    held_r,
     own_sem,
     w_sem,
     wx_s,
@@ -228,6 +229,26 @@
         t = chunk(c, wrap(major_at[c] - (1 - 2 * e) * s), wrap(minor_at[c] + minor_offset(j)))
         landed(g.at[c, t], flow_r.at[c, e, lax.rem(j, cycle), s - 1])
 
+    held = min(6, n)
+
+    def held_chunk(c, j, s):
+        return chunk(c, wrap(major_at[c] - (1 - 2 * (j % 2)) * s), wrap(minor_at[c] + minor_offset(j)))
+
+    def held_copy(c, j):
+        t = held_chunk(c, j, half - 1)
+        to = {major_axis[c]: wrap(major_at[c] + 1 - 2 * (j % 2))}
+        return remote(g.at[c, t], g.at[c, t], ag_s.at[c], held_r.at[c, j], to)
+
+    def held_send(first, stop):
+        for j in range(first, stop):
+            for c in range(2):
+                held_copy(c, j).start()
+
+    def held_landed():
+        for j in range(held):
+            for c in range(2):
+                landed(g.at[c, held_chunk(c, j, half)], held_r.at[c, j])
+
     def is_long(e, j):
         return lax.rem(j, 2) == e
 
@@ -238,9 +259,10 @@
         def _():
             lax.fori_loop(j, j + 1 + jnp.where(at == first, 1, 0), lambda k, z: (body(k), z)[1], 0)
 
-    def ag_tick(tick):
-        streams(tick, 1, ag1_step)
-        for s in range(half + 1):
+    def ag_tick(tick, steps):
+        if 0 in steps:
+            streams(tick, 1, ag1_step)
+        for s in steps:
 
             def hop(j, s=s):
                 for c in range(2):
@@ -252,12 +274,12 @@
                                 ag2_copy(c, e, j, s).start()
                             else:
 
-                                @pl.when(is_long(e, j))
+                                @pl.when(jnp.logical_and(is_long(e, j), j >= held))
                                 def _(c=c, e=e):
                                     ag2_copy(c, e, j, s).start()
                         else:
 
-                            @pl.when(is_long(e, j))
+                            @pl.when(jnp.logical_and(is_long(e, j), j >= held))
                             def _(c=c, e=e):
                                 ag2_landed(c, e, j, s)
 
@@ -334,8 +356,8 @@
                     total = total + get(r2, (c, k))
                 igrad[c] = total.astype(BF16)
 
-    def rs_tick(tick):
-        for s in range(half + 1):
+    def rs_tick(tick, steps):
+        for s in steps:
 
             def hop(i, s=s):
                 for c in range(2):
@@ -361,6 +383,9 @@
                     rs2_step(i)
 
             streams(tick - s, n - 3, hop)
+
+    def some(body, first, last):
+        lax.fori_loop(first, last, lambda k, z: (body(k), z)[1], 0)
 
     def member_of(b):
         end, count = jnp.int32(0), jnp.int32(0)
@@ -492,37 +517,57 @@
         for b in range(2):
             put(p, (b, t), out[b * BLOCK : (b + 1) * BLOCK])
 
-    def front_group(k):
-        first = k * group
+    far_row, far_col = wrap(y + half), wrap(x + half)
+
+    def front_group(row, q, hole):
+        first = row * n + q * group
+        there = [first + i for i in range(group)]
+        if hole:
+            there = [jnp.where(q * group + i == far_col, chunks, t) for i, t in enumerate(there)]
         rows_in = jnp.concatenate(
-            [jnp.concatenate([g[0, first + i], g[1, first + i]], axis=0) for i in range(group)], axis=1
+            [jnp.concatenate([g[0, first + i], g[1, t]], axis=0) for i, t in enumerate(there)], axis=1
         )
         at = pl.multiple_of(first * width, LANES)
         acc[...] += dot(w[:, pl.ds(at, group * width)], rows_in, NT)
+
+    def front_early(k):
+        front_group(wrap(far_row + 1 + lax.div(k, n // group)), lax.rem(k, n // group), True)
+
+    def front_late():
+        for q in range(n // group):
+            front_group(far_row, q, False)
+
+        def column(k):
+            t = wrap(far_row + k) * n + far_col
+            acc[:, BLOCK:] += dot(w_chunk(t), g[1, t], NT)
+
+        some(column, 1, n)
 
     def hidden_step():
         for b in range(2):
             cols = acc[:, b * BLOCK : (b + 1) * BLOCK]
             hidden[:, b * BLOCK : (b + 1) * BLOCK] = (cols * live(b, cols.shape, 1)).astype(BF16)
 
-    def some(body, first, last):
-        lax.fori_loop(first, last, lambda k, z: (body(k), z)[1], 0)
-
     rs_from = n - 1 if n >= 8 else n + 1
-    last = max(rs_from + ticks - 1, low_to + 2)
+    last = max(rs_from + ticks - 1, low_to + 2, rs_from + n + 1)
     back_from, back_ticks = early, rs_from - early
     back_each = -(-chunks // back_ticks)
     front_from, front_ticks = ticks, 3
-    front_each = -(-(chunks // group) // front_ticks)
+    fronts = (n - 1) * (n // group)
+    front_each = -(-fronts // front_ticks)
+    tail = rs_from + n - 1
+
+    def messages(tick, steps):
+        @pl.when(tick < ticks)
+        def _():
+            ag_tick(tick, steps)
+
+        @pl.when(tick >= rs_from)
+        def _():
+            rs_tick(tick - rs_from, steps)
 
     def every_tick(tick, carry):
-        @pl.when(tick < ticks)
-        def _():
-            ag_tick(tick)
-
-        @pl.when(tick >= rs_from)
-        def _():
-            rs_tick(tick - rs_from)
+        messages(tick, range(half - 1))
 
         @pl.when(tick == early - 1)
         def _():
@@ -537,21 +582,34 @@
                 take(k).wait()
             mask_step()
             acc[...] = jnp.zeros_like(acc)
+            g[1, chunks] = jnp.zeros(g.shape[2:], BF16)
 
         @pl.when(tick == low_from)
         def _():
             low_rank_start()
             w_local.wait()
+
+        @pl.when(tick == middle)
+        def _():
+            landed(w_half(1 - d), wx_r)
+
+        @pl.when(jnp.logical_and(tick >= back_from, tick < back_from + back_ticks))
+        def _():
+            first = (tick - back_from) * back_each
+            some(back_chunk, first, jnp.minimum(first + back_each, chunks))
+
+        @pl.when(jnp.logical_and(tick >= front_from, tick < front_from + front_ticks))
+        def _():
+            first = (tick - front_from) * front_each
+            some(front_early, first, jnp.minimum(first + front_each, fronts))
+
+        messages(tick, range(half - 1, half + 1))
 
         for k in range(3 * half + 1):
 
             @pl.when(tick == low_from + k)
             def _(k=k):
                 low_step(k)
-
-        @pl.when(tick == middle)
-        def _():
-            landed(w_half(1 - d), wx_r)
 
         @pl.when(tick == low_to)
         def _():
@@ -564,18 +622,18 @@
         def _():
             grads_done()
 
-        @pl.when(jnp.logical_and(tick >= back_from, tick < back_from + back_ticks))
-        def _():
-            first = (tick - back_from) * back_each
-            some(back_chunk, first, jnp.minimum(first + back_each, chunks))
-
-        @pl.when(jnp.logical_and(tick >= front_from, tick < front_from + front_ticks))
-        def _():
-            first = (tick - front_from) * front_each
-            some(front_group, first, jnp.minimum(first + front_each, chunks // group))
-
-        @pl.when(tick == front_from + front_ticks)
-        def _():
+        @pl.when(tick == tail)
+        def _():
+            held_send(0, 2)
+
+        @pl.when(tick == tail + 1)
+        def _():
+            held_send(2, held)
+
+        @pl.when(tick == tail + 2)
+        def _():
+            held_landed()
+            front_late()
             hidden_step()
 
         return carry
@@ -633,7 +691,7 @@
             pltpu.SMEM(member_blocks.shape, jnp.int32),
             pltpu.SMEM(block_live.shape, jnp.int32),
             pltpu.VMEM((hidden_width, token_rows), BF16),
-            pltpu.VMEM((blocks, chunks, BLOCK, width), BF16),
+            pltpu.VMEM((blocks, chunks + 1, BLOCK, width), BF16),
             pltpu.VMEM((hidden_width, chunks * width), BF16),
             pltpu.VMEM((blocks, chunks, coded, LANES), jnp.int32),
             pltpu.VMEM((*both_ways, coded, LANES), jnp.int32),
@@ -657,6 +715,7 @@
             dma(2),
             dma(2, 2, 5 if n >= 8 else 2 * n, half),
             dma(2, n),
+            dma(2, min(6, n)),
             pltpu.SemaphoreType.DMA,
             pltpu.SemaphoreType.DMA,
             pltpu.SemaphoreType.DMA,

time: 120 us -> 118 us (0.983)
  Pallas kernels: 120 us -> 117 us
    pallas_call x1, Pallas kernels: 119 us -> 116 us  [local(): pl.pallas_call(functools.partial(kernel, n), out_shape=(jax.ShapeDtypeStr...]
where the time goes in v6:
time: 118 us; the launch traced here: 117 us
  Pallas kernels  117 us (99%)
    pallas_call x1, Pallas kernels, local(): pl.pallas_call(functools.partial(kernel, n), out_shape=(jax.ShapeDtypeStr...  116 us

profile of v6, /device:TPU:514, one launch (start us, length us, event | category | flops | bytes accessed | tf_op | source)
XLA Modules:
  0.0 117.5 jit_solution(16663331178363409141)
XLA Ops:
  0.6 115.9 %step.1 = (bf16[416,256]{1,0:T(8,128)(2,1)S(1)}, bf16[2,128,256]{2,1,0:T(8,128)(2,1)S(1)}, f32[2,64,256]{2,1,0:T(8,128)S(1)}, f32[2,64,416]{2,1,0:T(8,128)S(1)}) custom-call(s32[4]{0:T(128)} %mb_hbm.1, s32[2]{0:T(128)} %bl_hbm.1, bf16[2,128,256]{2,1,0:T(8,128)(2,1)} %bitcast.9, bf16[416,8192]{1,0:T(8,128)(2,1)} %bitcast.7, bf16[2,64,256]{2,1,0:T(8,128)(2,1)} %bitcast.10, ...), custom_call_target="tpu_custom_call" | custom-call | tf_op jit(solution)/shard_map/step/pallas_call | solution.py:680
  116.6 0.9 hand_over.1

commit v7 on v6

--- a/solution.py
+++ b/solution.py
@@ -288,7 +288,7 @@
     def dest_offset(i):
         ahead = lax.div(n - i, 2)
         back = lax.div(n - 1 - i, 2)
-        return jnp.where(lax.rem(i, 2) == 0, ahead, -back)
+        return jnp.where(lax.rem(i, 2) == 0, -ahead, back)
 
     def hops(e, i):
         return jnp.where(is_long(e, i), half, half - 1)
@@ -341,11 +341,11 @@
 
             @pl.when(jnp.logical_and(i < n - 1, lax.rem(i, 2) == 0))
             def _(c=c):
-                rs2_copy(c, i, True).start()
+                rs2_copy(c, i, False).start()
 
             @pl.when(jnp.logical_and(i < n - 1, lax.rem(i, 2) == 1))
             def _(c=c):
-                rs2_copy(c, i, False).start()
+                rs2_copy(c, i, True).start()
 
             @pl.when(i == n - 1)
             def _(c=c):

time: 118 us -> 116 us (0.983)
  Pallas kernels: 117 us -> 115 us
    pallas_call x1, Pallas kernels: 116 us -> 114 us  [local(): pl.pallas_call(functools.partial(kernel, n), out_shape=(jax.ShapeDtypeStr...]
where the time goes in v7:
time: 116 us
  Pallas kernels  115 us (99%)
    pallas_call x1, Pallas kernels, local(): pl.pallas_call(functools.partial(kernel, n), out_shape=(jax.ShapeDtypeStr...  114 us

profile of v7, /device:TPU:514, one launch (start us, length us, event | category | flops | bytes accessed | tf_op | source)
XLA Modules:
  0.0 115.8 jit_solution(8546164206164462980)
XLA Ops:
  0.6 114.3 %step.1 = (bf16[416,256]{1,0:T(8,128)(2,1)S(1)}, bf16[2,128,256]{2,1,0:T(8,128)(2,1)S(1)}, f32[2,64,256]{2,1,0:T(8,128)S(1)}, f32[2,64,416]{2,1,0:T(8,128)S(1)}) custom-call(s32[4]{0:T(128)} %mb_hbm.1, s32[2]{0:T(128)} %bl_hbm.1, bf16[2,128,256]{2,1,0:T(8,128)(2,1)} %bitcast.9, bf16[416,8192]{1,0:T(8,128)(2,1)} %bitcast.7, bf16[2,64,256]{2,1,0:T(8,128)(2,1)} %bitcast.10, ...), custom_call_target="tpu_custom_call" | custom-call | tf_op jit(solution)/shard_map/step/pallas_call | solution.py:680
  114.9 0.9 hand_over.1

commit v8 on v7

--- a/solution.py
+++ b/solution.py
@@ -511,11 +511,13 @@
             ugrad[q] = ugrad[q] + urecv[q]
             dgrad[q] = dgrad[q] + drecv[q]
 
-    def back_chunk(k):
-        t = lax.rem(d * own_chunks + k, chunks)
-        out = dot(masked[...], w_chunk(t), NN)
-        for b in range(2):
-            put(p, (b, t), out[b * BLOCK : (b + 1) * BLOCK])
+    def back_pair(k):
+        t = lax.rem(d * own_chunks + 2 * k, chunks)
+        at = pl.multiple_of(t * width, LANES)
+        out = dot(masked[...], w[:, pl.ds(at, 2 * width)], NN)
+        for i in range(2):
+            for b in range(2):
+                put(p, (b, t + i), out[b * BLOCK : (b + 1) * BLOCK, i * width : (i + 1) * width])
 
     far_row, far_col = wrap(y + half), wrap(x + half)
 
@@ -551,7 +553,7 @@
     rs_from = n - 1 if n >= 8 else n + 1
     last = max(rs_from + ticks - 1, low_to + 2, rs_from + n + 1)
     back_from, back_ticks = early, rs_from - early
-    back_each = -(-chunks // back_ticks)
+    back_each = -(-(chunks // 2) // back_ticks)
     front_from, front_ticks = ticks, 3
     fronts = (n - 1) * (n // group)
     front_each = -(-fronts // front_ticks)
@@ -596,7 +598,7 @@
         @pl.when(jnp.logical_and(tick >= back_from, tick < back_from + back_ticks))
         def _():
             first = (tick - back_from) * back_each
-            some(back_chunk, first, jnp.minimum(first + back_each, chunks))
+            some(back_pair, first, jnp.minimum(first + back_each, chunks // 2))
 
         @pl.when(jnp.logical_and(tick >= front_from, tick < front_from + front_ticks))
         def _():

time: 116 us -> 115 us (level)
    pallas_call x1, Pallas kernels: 114 us -> 113 us  [local(): pl.pallas_call(functools.partial(kernel, n), out_shape=(jax.ShapeDtypeStr...]
where the time goes in v8:
time: 115 us; the launch traced here: 114 us
  Pallas kernels  114 us (99%)
    pallas_call x1, Pallas kernels, local(): pl.pallas_call(functools.partial(kernel, n), out_shape=(jax.ShapeDtypeStr...  113 us

profile of v8, /device:TPU:514, one launch (start us, length us, event | category | flops | bytes accessed | tf_op | source)
XLA Modules:
  0.0 114.5 jit_solution(10599616264479677028)
XLA Ops:
  0.6 112.9 %step.1 = (bf16[416,256]{1,0:T(8,128)(2,1)S(1)}, bf16[2,128,256]{2,1,0:T(8,128)(2,1)S(1)}, f32[2,64,256]{2,1,0:T(8,128)S(1)}, f32[2,64,416]{2,1,0:T(8,128)S(1)}) custom-call(s32[4]{0:T(128)} %mb_hbm.1, s32[2]{0:T(128)} %bl_hbm.1, bf16[2,128,256]{2,1,0:T(8,128)(2,1)} %bitcast.9, bf16[416,8192]{1,0:T(8,128)(2,1)} %bitcast.7, bf16[2,64,256]{2,1,0:T(8,128)(2,1)} %bitcast.10, ...), custom_call_target="tpu_custom_call" | custom-call | tf_op jit(solution)/shard_map/step/pallas_call | solution.py:682
  113.6 0.9 hand_over.1
